TPU v7x, 128 devices: a whole 4x4x4 slice. The times are simulated.
128 devices in a mesh: sub: 32 (over z, y, core), rve: 4 (over x).
Axes of the slice: x: 4, y: 4, z: 4, core: 2. Of those that a mesh axis runs over, the one named last changes fastest.
Arguments:
- displacement: float32 [3, 32, 8, 8], P(None, 'sub', 'rve'), may hold values from -4 to 4
- load: float32 [3, 32, 8, 8], P(None, 'sub', 'rve'), may hold values from -6 to 6
- home_slot: int32 [16384], P(('sub', 'rve')), may hold values from 0 to 16383, as said below
- micro_state: float32 [7, 3, 216, 16384], P(None, None, None, ('sub', 'rve')), may hold values from -6 to 6
- state_slot: int32 [16384], P(('sub', 'rve')), may hold values from 0 to 16383, as said below
- phases: int32 [216, 16384], P(None, ('sub', 'rve')), may hold values from 0 to 2
- phase_moduli: float32 [2, 3], replicated, may hold values from 0.5 to 8
Outputs:
- new_state: float32 [7, 3, 216, 16384], P(None, None, None, ('sub', 'rve'))
- displaced: float32 [3, 32, 8, 8], P(None, 'sub', 'rve')
- residual: float32 [3, 32, 8, 8], P(None, 'sub', 'rve')
- rel_norm: float32 [], replicated
Inputs may be any that keep to these rules, and one draw needn't show every extreme that they name: `home_slot`: A permutation of 0 to 16383. The 128 entries held by device s (devices numbered in sub+rve order) contain, for every device d, exactly one value, d * 128 + s, in an order drawn at random; so each device sends exactly one Gauss point to every device. `state_slot`: A permutation of 0 to 16383 with the same structure: the 128 entries held by device s contain, for every device d, exactly one value, d * 128 + s, in an order drawn at random.
All inputs are finite; a program needn't handle non-finite values.
Results may differ from a plain program's by a relative error of at most 0.0003.
Values sent between devices are 32-bit elements; how exact they have to be, the bound alone decides.
No kernel may reach another device: no remote copies, remote signals or barrier semaphores. Data moves between devices by JAX's collectives and lax.ppermute only.
A program may use at most 128 MiB of HBM per device.

v0:
```python
import math

import jax
import jax.numpy as jnp
import numpy as np
from jax import lax
from jax.experimental import pallas as pl
from jax.experimental.pallas import tpu as pltpu
from jax.sharding import PartitionSpec as P

R = 6
VOX = R * R * R
ROWS = 3 * VOX
CASES = 7
DEV = 128
LANES = 128
CHUNKS = 36
WIDE = CHUNKS * LANES
TAIL = CASES * ROWS - (CHUNKS - 1) * LANES
NODES = 48
STAB = 0.1
FLOOR = 1.0
AXES = ("sub", "rve")
PAIRS = ((0, 5, 4), (5, 1, 3), (4, 3, 2))
STRAIN_OF = ((0, 4, 5), (5, 1, 3), (4, 3, 2))
OFF_DIAGONAL = ((0, 4), (0, 5), (4, 5), (1, 3), (1, 5), (3, 5), (2, 3), (2, 4), (3, 4))
LOW = 0.5 - 0.5 / math.sqrt(3.0)
HIGH = 0.5 + 0.5 / math.sqrt(3.0)
HIGHEST = lax.Precision.HIGHEST
VMEM = pl.BlockSpec(memory_space=pltpu.VMEM)
SMEM = pl.BlockSpec(memory_space=pltpu.SMEM)


def strain_table():
    places = (LOW, HIGH)
    table = np.zeros((8, 8, 3, 6))
    for gauss in range(8):
        at = (places[gauss % 2], places[gauss // 2 % 2], places[gauss // 4])
        for corner in range(8):
            bits = (corner % 2, corner // 2 % 2, corner // 4)
            weight = [at[k] if bits[k] else 1.0 - at[k] for k in range(3)]
            sign = [1.0 if bits[k] else -1.0 for k in range(3)]
            dx = sign[0] * weight[1] * weight[2]
            dy = weight[0] * sign[1] * weight[2]
            dz = weight[0] * weight[1] * sign[2]
            table[gauss, corner, 0, [0, 4, 5]] = (dx, dz, dy)
            table[gauss, corner, 1, [1, 3, 5]] = (dy, dz, dx)
            table[gauss, corner, 2, [2, 3, 4]] = (dz, dy, dx)
    return table


def term_index(first, second):
    if first == second:
        return first
    return 6 + OFF_DIAGONAL.index((min(first, second), max(first, second)))


def diagonal_terms(component):
    m = STRAIN_OF[component]
    pairs = [(m[0], m[0]), (m[1], m[1]), (m[2], m[2]), (m[0], m[1]), (m[0], m[2]), (m[1], m[2])]
    return [(a, b, term_index(a, b)) for a, b in pairs]


def assembly_tables():
    table = strain_table()
    force = np.zeros((6, LANES, 2 * LANES), np.float32)
    weights = np.zeros((3, 6, 8, LANES), np.float32)
    place = np.zeros((4, LANES, LANES), np.float32)
    for j in range(LANES):
        ly, ex, gauss = j // 64, j // 8 % 8, j % 8
        for corner in range(8):
            az, row, col = corner // 4, ly + corner // 2 % 2, (ex + corner % 2) % 8
            for i in range(3):
                lane = az * LANES + (NODES if row == 2 else 0) + i * 16 + row % 2 * 8 + col
                for m in STRAIN_OF[i]:
                    force[m, j, lane] += 0.125 * table[gauss, corner, i, m]
                for n, (first, second, _) in enumerate(diagonal_terms(i)):
                    weights[i, n, corner, j] = (
                        0.125 * table[gauss, corner, i, first] * table[gauss, corner, i, second]
                    )
            place[az * 2 + (1 if row == 2 else 0), j, corner * 16 + row % 2 * 8 + col] = 1.0
    return force.reshape(6 * LANES, 2 * LANES), weights.reshape(18 * 8, LANES), place


def lane_iota(rows=1):
    return lax.broadcasted_iota(jnp.int32, (rows, LANES), 1)


def sublane_iota(rows=8):
    return lax.broadcasted_iota(jnp.int32, (rows, LANES), 0)


def node_row(ref, scratch, offset):
    scratch[...] = jnp.zeros((8, LANES), jnp.float32)
    for i in range(3):
        scratch[2 * i : 2 * i + 2, 0:8] = ref[i, 0]
    tile = scratch[...]
    total = jnp.zeros((1, LANES), jnp.float32)
    for row in range(6):
        total = total + pltpu.roll(tile[row : row + 1], offset + 8 * row, 1)
    return total


def previous_row_lanes(value):
    lane = lane_iota(value.shape[0])
    return jnp.where(lane % 4 == 0, pltpu.roll(value, LANES - 3, 1), pltpu.roll(value, 1, 1))


def next_row_lanes(value):
    lane = lane_iota(value.shape[0])
    return jnp.where(lane % 4 == 3, pltpu.roll(value, 3, 1), pltpu.roll(value, LANES - 1, 1))


def below_lanes(value):
    return jnp.where(lane_iota(value.shape[0]) < 4, 0.0, pltpu.roll(value, 4, 1))


def above_lanes(value):
    return jnp.where(lane_iota(value.shape[0]) >= 124, 0.0, pltpu.roll(value, LANES - 4, 1))


def pack_kernel(state_ref, state_slot_ref, home_slot_ref, disp_ref, out_ref, scratch):
    owner = sublane_iota(DEV)
    lane = lane_iota(DEV)
    chosen = (state_slot_ref[...] >> 7) == owner
    choose = chosen.astype(jnp.float32)
    for k in range(CHUNKS):
        if k < CHUNKS - 1:
            block = state_ref[k * LANES : (k + 1) * LANES, :]
        else:
            block = jnp.concatenate(
                [
                    state_ref[k * LANES : k * LANES + TAIL, :],
                    jnp.zeros((LANES - TAIL, LANES), jnp.float32),
                ],
                axis=0,
            )
        turned = lax.dot_general(
            choose,
            block,
            (((1,), (1,)), ((), ())),
            precision=HIGHEST,
            preferred_element_type=jnp.float32,
        )
        if k == CHUNKS - 1:
            home = (home_slot_ref[...] >> 7) == owner
            local = jnp.sum(jnp.where(home, lane, 0).astype(jnp.float32), axis=1, keepdims=True)
            extra = node_row(disp_ref, scratch, TAIL)
            turned = turned + extra + jnp.where(lane == TAIL + NODES, local, 0.0)
        out_ref[:, 0, k * LANES : (k + 1) * LANES] = turned


def macro_strain_rows(tail):
    local = tail[TAIL + NODES : TAIL + NODES + 1].astype(jnp.int32)
    upper = (local >> 6) == 1
    ex = (local >> 3) & 7
    point = [jnp.where(((local >> k) & 1) == 1, HIGH, LOW) for k in range(3)]
    shape = [(1.0 - point[k], point[k]) for k in range(3)]
    sub = sublane_iota()
    hits = (sub == ex, sub == ((ex + 1) & 7))
    slopes = []
    for i in range(3):
        own = [tail[TAIL + 16 * i + 8 * y : TAIL + 16 * i + 8 * y + 8] for y in range(2)]
        rows = [own[0], own[1], next_row_lanes(own[0])]
        planes = [rows, [above_lanes(row) for row in rows]]
        at = {}
        for az in range(2):
            for ay in range(2):
                chosen = jnp.where(upper, planes[az][ay + 1], planes[az][ay])
                for ax in range(2):
                    at[az, ay, ax] = jnp.sum(
                        jnp.where(hits[ax], chosen, 0.0), axis=0, keepdims=True
                    )
        sx, sy, sz = shape
        slope = [0.0, 0.0, 0.0]
        for first in range(2):
            for second in range(2):
                slope[0] = slope[0] + sz[first] * sy[second] * (
                    at[first, second, 1] - at[first, second, 0]
                )
                slope[1] = slope[1] + sz[first] * sx[second] * (
                    at[first, 1, second] - at[first, 0, second]
                )
                slope[2] = slope[2] + sy[first] * sx[second] * (
                    at[1, first, second] - at[0, first, second]
                )
        slopes.append(slope)
    return [
        slopes[0][0],
        slopes[1][1],
        slopes[2][2],
        slopes[1][2] + slopes[2][1],
        slopes[0][2] + slopes[2][0],
        slopes[0][1] + slopes[1][0],
    ]


def tile_at(ref, base, row):
    return ref[pl.ds(base + row * 8, 8), :]


def solve_kernel(
    recv_ref,
    phase_ref,
    moduli_ref,
    slot_ref,
    load_ref,
    ret_ref,
    w_ref,
    p_ref,
    q_ref,
    step_ref,
    sig_ref,
    lam_ref,
    mu_ref,
    mu2_ref,
    scratch,
):
    zero = jnp.zeros((8, LANES), jnp.float32)
    phase = phase_ref[...]
    mu = jnp.where(
        phase == 0, moduli_ref[1, 0], jnp.where(phase == 1, moduli_ref[1, 1], moduli_ref[1, 2])
    )
    lam_ref[...] = jnp.where(
        phase == 0, moduli_ref[0, 0], jnp.where(phase == 1, moduli_ref[0, 1], moduli_ref[0, 2])
    )
    mu_ref[...] = mu
    mu2_ref[...] = mu + mu
    w_ref[pl.ds(7, ROWS, stride=8), :] = jnp.zeros((ROWS, LANES), jnp.float32)
    tail = None
    for k in range(CHUNKS):
        turned = recv_ref[:, 0, k * LANES : (k + 1) * LANES].T
        start, stop = k * LANES, min((k + 1) * LANES, CASES * ROWS)
        while start < stop:
            case = start // ROWS
            end = min(stop, (case + 1) * ROWS)
            w_ref[pl.ds((start - case * ROWS) * 8 + case, end - start, stride=8), :] = turned[
                start - k * LANES : end - k * LANES
            ]
            start = end
        tail = turned
    macro = macro_strain_rows(tail)
    sub = sublane_iota()
    imposed = [
        jnp.where(sub == 0, macro[m], jnp.where(sub == m + 1, 1.0, 0.0)) for m in range(6)
    ]

    def stress_pass(src, strain, keep, energy):
        def plane(a, carry):
            sums, work = list(carry[0]), carry[1]
            base = pl.multiple_of(a * 288, 8)
            ahead = pl.multiple_of(jnp.where(a == R - 1, 0, (a + 1) * 288), 8)
            voxel = a * 36
            line = [[tile_at(src, base, i * VOX + c) for c in range(R)] for i in range(3)]
            for b in range(R):
                nb = (b + 1) % R
                below = [
                    [tile_at(src, base, i * VOX + nb * R + c) for c in range(R)] for i in range(3)
                ]
                for c in range(R):
                    at = b * R + c
                    here = [line[i][c] for i in range(3)]
                    grad = [
                        [
                            tile_at(src, ahead, i * VOX + at) - here[i],
                            below[i][c] - here[i],
                            line[i][(c + 1) % R] - here[i],
                        ]
                        for i in range(3)
                    ]
                    eps = [
                        grad[0][0],
                        grad[1][1],
                        grad[2][2],
                        grad[1][2] + grad[2][1],
                        grad[0][2] + grad[2][0],
                        grad[0][1] + grad[1][0],
                    ]
                    if strain is not None:
                        eps = [eps[m] + strain[m] for m in range(6)]
                    lam = lam_ref[pl.ds(voxel + at, 8, stride=0), :]
                    mu1 = mu_ref[pl.ds(voxel + at, 8, stride=0), :]
                    mu2 = mu2_ref[pl.ds(voxel + at, 8, stride=0), :]
                    bulk = lam * (eps[0] + eps[1] + eps[2])
                    sig = [bulk + mu2 * eps[m] for m in range(3)]
                    sig += [mu1 * eps[m] for m in range(3, 6)]
                    for m in range(6):
                        sums[m] = sums[m] + sig[m]
                        if keep:
                            sig_ref[pl.ds(base + (m * VOX + at) * 8, 8), :] = sig[m]
                    if energy:
                        work = work + (
                            (sig[0] * eps[0] + sig[1] * eps[1])
                            + (sig[2] * eps[2] + sig[3] * eps[3])
                            + (sig[4] * eps[4] + sig[5] * eps[5])
                        )
                line = below
            return tuple(sums), work

        return lax.fori_loop(0, R, plane, ((zero,) * 6, zero))

    def force_pass(src, finish, dst):
        def plane(a, total):
            base = pl.multiple_of(a * 288, 8)
            behind = pl.multiple_of(jnp.where(a == 0, (R - 1) * 288, (a - 1) * 288), 8)
            for b in range(R):
                pb = (b + R - 1) % R
                last = [tile_at(sig_ref, base, PAIRS[2][i] * VOX + b * R + R - 1) for i in range(3)]
                for c in range(R):
                    at = b * R + c
                    own = [tile_at(sig_ref, base, m * VOX + at) for m in range(6)]
                    for i in range(3):
                        gone = (own[PAIRS[0][i]] + own[PAIRS[1][i]]) + own[PAIRS[2][i]]
                        come = (
                            tile_at(sig_ref, behind, PAIRS[0][i] * VOX + at)
                            + tile_at(sig_ref, base, PAIRS[1][i] * VOX + pb * R + c)
                        ) + last[i]
                        value = finish(come - gone, tile_at(src, base, i * VOX + at))
                        dst[pl.ds(base + (i * VOX + at) * 8, 8), :] = value
                        total = total + value * value
                    last = [own[PAIRS[2][i]] for i in range(3)]
            return total

        return lax.fori_loop(0, R, plane, zero)

    mean0, _ = stress_pass(w_ref, imposed, True, False)
    square0 = force_pass(w_ref, lambda div, w: -(div + STAB * w), p_ref)
    mean1, work1 = stress_pass(p_ref, None, True, True)
    step0 = square0 / (work1 + STAB * square0)
    square1 = force_pass(p_ref, lambda div, p: p - step0 * (div + STAB * p), q_ref)
    ratio = square1 / square0

    def direction(a, total):
        base = pl.multiple_of(a * 288, 8)
        for i in range(3):
            for at in range(36):
                value = tile_at(q_ref, base, i * VOX + at) + ratio * tile_at(
                    p_ref, base, i * VOX + at
                )
                q_ref[pl.ds(base + (i * VOX + at) * 8, 8), :] = value
                total = total + value * value
        return total

    length = lax.fori_loop(0, R, direction, zero)
    mean2, work2 = stress_pass(q_ref, None, False, True)
    step1 = square1 / (work2 + STAB * length)
    step_ref[0:8, :] = step0
    step_ref[8:16, :] = step1
    mean = [(mean0[m] + step0 * mean1[m] + step1 * mean2[m]) * (1.0 / VOX) for m in range(6)]

    shared = (slot_ref[...] >> 7).astype(jnp.float32)
    shared = jnp.broadcast_to(shared, (8, LANES))
    for m in range(6):
        shared = jnp.where(sub == m, mean[m][0:1], shared)
    terms = [mean[m][m + 1 : m + 2] for m in range(6)]
    for first, second in OFF_DIAGONAL:
        terms.append(mean[first][second + 1 : second + 2] + mean[second][first + 1 : first + 2])
    own = jnp.concatenate(terms + [jnp.zeros((1, LANES), jnp.float32)], axis=0)
    left = previous_row_lanes(own)
    stacked = jnp.concatenate(
        [jnp.zeros((64, LANES), jnp.float32), own, left, below_lanes(own), below_lanes(left)],
        axis=0,
    )
    special = stacked.T + node_row(load_ref, scratch, 0)
    for peer in range(DEV):
        ret_ref[8 * peer : 8 * peer + 8, :] = shared
    ret_ref[pl.ds(7, DEV, stride=8), :] = special


def update_kernel(w_ref, p_ref, q_ref, step_ref, out_ref):
    for case in range(CASES):
        first = step_ref[case : case + 1, :]
        second = step_ref[8 + case : 9 + case, :]
        for start in range(0, ROWS, 72):
            rows = pl.ds(start * 8 + case, 72, stride=8)
            out_ref[case * ROWS + start : case * ROWS + start + 72, :] = (
                w_ref[rows, :] + first * p_ref[rows, :] + second * q_ref[rows, :]
            )


def row_of(value, index):
    return jnp.sum(jnp.where(sublane_iota(DEV) == index, value, 0), axis=0, keepdims=True)


def node_tile(row):
    sub = sublane_iota()
    wide = jnp.broadcast_to(row, (8, LANES))
    tile = wide
    for r in range(1, 6):
        tile = jnp.where(sub == r, pltpu.roll(wide, LANES - 8 * r, 1), tile)
    return tile


def final_kernel(
    recv_ref,
    me_ref,
    disp_ref,
    force_ref,
    weight_ref,
    place_ref,
    new_disp_ref,
    res_ref,
    norm_ref,
    scratch,
):
    me = me_ref[0, 0]
    order = recv_ref[pl.ds(6, DEV, stride=8), :].astype(jnp.int32)
    special = recv_ref[pl.ds(7, DEV, stride=8), :]
    stress = [
        jnp.take_along_axis(recv_ref[pl.ds(m, DEV, stride=8), :].T, order, axis=1)
        for m in range(6)
    ]
    forces = lax.dot_general(
        jnp.concatenate(stress, axis=1),
        force_ref[...],
        (((1,), (0,)), ((), ())),
        precision=HIGHEST,
        preferred_element_type=jnp.float32,
    )
    home = sublane_iota(DEV)
    lifted = jnp.where(home < 4, 0.0, pltpu.roll(forces[:, LANES:], 4, 0))
    near = forces[:, :LANES] + lifted
    beside = jnp.where(home % 4 == 0, pltpu.roll(near, DEV - 3, 0), pltpu.roll(near, 1, 0))
    force = near + pltpu.roll(beside, LANES - NODES, 1)
    node = lane_iota(DEV) < NODES
    loads = jnp.where(node, special, 0.0)
    residual = jnp.where(node, special - force, 0.0)
    top = jnp.sum(jnp.sum(residual * residual, axis=0, keepdims=True), axis=1, keepdims=True)
    bottom = jnp.sum(jnp.sum(loads * loads, axis=0, keepdims=True), axis=1, keepdims=True)
    norm_ref[...] = jnp.sqrt(top / bottom)

    own_residual = row_of(residual, me)
    left = jnp.where(me % 4 == 0, me + 3, me - 1)
    under = jnp.where(me < 4, 0, 4)
    turned = special.T
    diagonal = jnp.zeros((24, LANES), jnp.float32)
    for k, source in enumerate((me, left, me - under, left - under)):
        picks = jnp.broadcast_to(row_of(order, source), (16, LANES))
        terms = jnp.take_along_axis(turned[64 + 16 * k : 80 + 16 * k], picks, axis=1)
        corner = []
        for i in range(3):
            total = jnp.zeros((8, LANES), jnp.float32)
            for n, (_, _, t) in enumerate(diagonal_terms(i)):
                at = (i * 6 + n) * 8
                total = total + weight_ref[at : at + 8, :] * terms[t : t + 1]
            corner.append(total)
        diagonal = diagonal + lax.dot_general(
            jnp.concatenate(corner, axis=0),
            place_ref[k],
            (((1,), (0,)), ((), ())),
            precision=HIGHEST,
            preferred_element_type=jnp.float32,
        )
    lane = lane_iota(8)
    same = lane // 16 == sublane_iota()
    row = jnp.zeros((1, LANES), jnp.float32)
    for i in range(3):
        part = jnp.sum(jnp.where(same, diagonal[8 * i : 8 * i + 8], 0.0), axis=0, keepdims=True)
        for shift in (64, 32, 16):
            part = part + pltpu.roll(part, shift, 1)
        row = jnp.where(lane_iota() // 16 == i, part, row)
    moved = node_row(disp_ref, scratch, 0) + own_residual / jnp.maximum(row, FLOOR)
    for value, ref in ((moved, new_disp_ref), (own_residual, res_ref)):
        tile = node_tile(value)
        for i in range(3):
            ref[i, 0] = tile[2 * i : 2 * i + 2, 0:8]


def exchange(value):
    return lax.all_to_all(value, AXES, split_axis=0, concat_axis=0, tiled=True)


def per_device(displacement, load, home_slot, micro_state, state_slot, phases, phase_moduli):
    force_table, weight_table, place_table = assembly_tables()
    f32 = jnp.float32
    home_row = home_slot.reshape(1, LANES)
    sent = pl.pallas_call(
        pack_kernel,
        out_shape=jax.ShapeDtypeStruct((DEV, 1, WIDE), f32),
        in_specs=[VMEM] * 4,
        out_specs=VMEM,
        scratch_shapes=[pltpu.VMEM((8, LANES), f32)],
        name="pack",
    )(
        micro_state.reshape(CASES * ROWS, LANES),
        state_slot.reshape(1, LANES),
        home_row,
        displacement,
    )
    received = exchange(sent)
    big = jax.ShapeDtypeStruct((ROWS * 8, LANES), f32)
    answer, w, p, q, steps = pl.pallas_call(
        solve_kernel,
        out_shape=(
            jax.ShapeDtypeStruct((DEV * 8, LANES), f32),
            big,
            big,
            big,
            jax.ShapeDtypeStruct((16, LANES), f32),
        ),
        in_specs=[VMEM, VMEM, SMEM, VMEM, VMEM],
        out_specs=[VMEM] * 5,
        scratch_shapes=[
            pltpu.VMEM((6 * VOX * 8, LANES), f32),
            pltpu.VMEM((VOX, LANES), f32),
            pltpu.VMEM((VOX, LANES), f32),
            pltpu.VMEM((VOX, LANES), f32),
            pltpu.VMEM((8, LANES), f32),
        ],
        name="solve",
    )(received, phases, phase_moduli, home_row, load)
    returned = exchange(answer.reshape(DEV, 8, LANES)).reshape(DEV * 8, LANES)
    new_state = pl.pallas_call(
        update_kernel,
        out_shape=jax.ShapeDtypeStruct((CASES * ROWS, LANES), f32),
        in_specs=[VMEM] * 4,
        out_specs=VMEM,
        cost_estimate=pl.CostEstimate(
            flops=20_000_000, bytes_accessed=10_000_000, transcendentals=0
        ),
        name="update",
    )(w, p, q, steps)
    me = lax.axis_index(AXES).astype(jnp.int32).reshape(1, 1)
    node_shape = jax.ShapeDtypeStruct(displacement.shape, f32)
    displaced, residual, rel_norm = pl.pallas_call(
        final_kernel,
        out_shape=(node_shape, node_shape, jax.ShapeDtypeStruct((1, 1), f32)),
        in_specs=[VMEM, SMEM, VMEM, VMEM, VMEM, VMEM],
        out_specs=[VMEM] * 3,
        scratch_shapes=[pltpu.VMEM((8, LANES), f32)],
        name="final",
    )(
        returned,
        me,
        displacement,
        jnp.asarray(force_table),
        jnp.asarray(weight_table),
        jnp.asarray(place_table),
    )
    return (
        new_state.reshape(micro_state.shape),
        displaced,
        residual,
        rel_norm.reshape(()),
    )


def solution(mesh):
    return jax.shard_map(
        per_device,
        mesh=mesh,
        in_specs=(
            P(None, "sub", "rve", None),
            P(None, "sub", "rve", None),
            P(AXES),
            P(None, None, None, AXES),
            P(AXES),
            P(None, AXES),
            P(),
        ),
        out_specs=(
            P(None, None, None, AXES),
            P(None, "sub", "rve", None),
            P(None, "sub", "rve", None),
            P(),
        ),
        check_vma=False,
    )
```

profile of v0, /device:TPU:1, one launch (start us, length us, event | category | flops | bytes accessed | tf_op | source)
XLA Modules:
  0.0 88.3 jit_solution(15541804140980776780)
XLA Ops:
  0.6 8.0 %pack.1 = f32[128,1,4608]{2,1,0:T(1,128)} custom-call(f32[4536,128]{1,0:T(8,128)} %bitcast.9, s32[1,128]{1,0:T(1,128)} %bitcast.14, s32[1,128]{1,0:T(1,128)} %bitcast.12, f32[3,1,2,8]{3,2,1,0:T(2,128)} %disp_ref.3), custom_call_target="tpu_custom_call" | custom-call | tf_op jit(solution)/shard_map/pack/pallas_call | solution.py:477
  8.6 45.2 %all_to_all.10.recv_ref = f32[128,1,4608]{2,1,0:T(1,128)} all-to-all(f32[128,1,4608]{2,1,0:T(1,128)} %pack.1), channel_id=1, replica_groups=mesh['sub'=32,'rve'=4] {'sub','rve'}, dimensions={0} | all-to-all | bytes 4718592 | tf_op jit(solution)/shard_map/all_to_all | solution.py:470
  53.8 12.8 %solve.1 = (f32[1024,128]{1,0:T(8,128)}, f32[5184,128]{1,0:T(8,128)}, f32[5184,128]{1,0:T(8,128)}, f32[5184,128]{1,0:T(8,128)}, f32[16,128]{1,0:T(8,128)}) custom-call(f32[128,1,4608]{2,1,0:T(1,128)} %all_to_all.10.recv_ref, s32[216,128]{1,0:T(8,128)} %phase_ref.1, f32[2,3]{1,0:T(2,128)} %moduli_ref.1, s32[1,128]{1,0:T(1,128)} %bitcast.13, ...), custom_call_target="tpu_custom_call" | custom-call | tf_op jit(solution)/shard_map/solve/pallas_call | solution.py:492
  66.5 3.8 %all-to-all-start.1 = ((f32[128,8,128]{2,1,0:T(8,128)}), f32[128,8,128]{2,1,0:T(8,128)S(1)}, u32[]{:S(2)}, u32[]{:S(2)}) async-start(f32[128,8,128]{2,1,0:T(8,128)} %bitcast.11), calls=%async_computation.1 | async-start | bytes 1048576 | tf_op jit(solution)/shard_map/all_to_all | solution.py:470
  70.3 6.5 %update.1 = f32[4536,128]{1,0:T(8,128)} custom-call(f32[5184,128]{1,0:T(8,128)} %get-tuple-element.12.w_ref, f32[5184,128]{1,0:T(8,128)} %get-tuple-element.13.p_ref, f32[5184,128]{1,0:T(8,128)} %get-tuple-element.14.q_ref, f32[16,128]{1,0:T(8,128)} %get-tuple-element.15.step_ref), custom_call_target="tpu_custom_call" | custom-call | flops 20000000 | bytes 10000000 | tf_op jit(solution)/shard_map/update/pallas_call | solution.py:513
  76.8 7.6 %all-to-all-done.1 = f32[128,8,128]{2,1,0:T(8,128)S(1)} async-done(((f32[128,8,128]{2,1,0:T(8,128)}), f32[128,8,128]{2,1,0:T(8,128)S(1)}, u32[]{:S(2)}, u32[]{:S(2)}) %all-to-all-start.1) | async-done | bytes 524320 | tf_op jit(solution)/shard_map/all_to_all | solution.py:470
  84.3 0.0 copy-start
  84.3 0.8 copy-done
  85.1 3.2 %final.1 = (f32[3,1,2,8]{3,2,1,0:T(2,128)}, f32[3,1,2,8]{3,2,1,0:T(2,128)}, f32[1,1]{1,0:T(1,128)}) custom-call(f32[1024,128]{1,0:T(8,128)} %bitcast.10, s32[1,1]{1,0:T(1,128)} %bitcast.6.me_ref, f32[3,1,2,8]{3,2,1,0:T(2,128)} %disp_ref.3, f32[768,256]{1,0:T(8,128)} %constant.17.clone.force_ref, f32[144,128]{1,0:T(8,128)} %constant.18.clone.weight_ref, ...), custom_call_target="tpu_custom_call" | custom-call | tf_op jit(solution)/shard_map/final/pallas_call | solution.py:525
Async XLA Ops:
  66.5 17.8 %all-to-all-start.1 = ((f32[128,8,128]{2,1,0:T(8,128)}), f32[128,8,128]{2,1,0:T(8,128)S(1)}, u32[]{:S(2)}, u32[]{:S(2)}) async-start(f32[128,8,128]{2,1,0:T(8,128)} %bitcast.11), calls=%async_computation.1 | async-start | bytes 1048576 | tf_op jit(solution)/shard_map/all_to_all | solution.py:470
  84.3 0.8 copy-start
where the time goes:
time: 88.6 us; the launch traced here: 88.3 us
  blocking collectives  45.2 us (51%)
  Pallas kernels  30.4 us (34%)
  waiting for transfers between devices  7.56 us (9%)
  starting transfers between devices  3.75 us (4%)
    all_to_all x1, blocking collectives, exchange(): return lax.all_to_all(value, AXES, split_axis=0, concat_axis=0, tiled=True)  45.2 us
    pallas_call x1, Pallas kernels, per_device(): pl.pallas_call(solve_kernel, out_shape=(jax.ShapeDtypeStruct((DEV * 8, LA...  12.8 us
    pallas_call x1, Pallas kernels, per_device(): pl.pallas_call(pack_kernel, out_shape=jax.ShapeDtypeStruct((DEV, 1, WIDE)...  7.96 us
    all_to_all x1, waiting for transfers between devices, exchange(): return lax.all_to_all(value, AXES, split_axis=0, concat_axis=0, tiled=True)  7.56 us
    pallas_call x1, Pallas kernels, per_device(): pl.pallas_call(update_kernel, out_shape=jax.ShapeDtypeStruct((CASES * ROW...  6.48 us
    all_to_all x1, starting transfers between devices, exchange(): return lax.all_to_all(value, AXES, split_axis=0, concat_axis=0, tiled=True)  3.75 us
    pallas_call x1, Pallas kernels, per_device(): pl.pallas_call(final_kernel, out_shape=(node_shape, node_shape, jax.Shape...  3.18 us
  transfers between devices with their start and end apart: 1, of which 1 were waited for; matrix products, arithmetic and copies ran while one was open for 0% of the time, Pallas kernels for 7%

commit v1 on v0

--- a/solution.py
+++ b/solution.py
@@ -29,6 +29,10 @@
 HIGHEST = lax.Precision.HIGHEST
 VMEM = pl.BlockSpec(memory_space=pltpu.VMEM)
 SMEM = pl.BlockSpec(memory_space=pltpu.SMEM)
+HBM = pl.BlockSpec(memory_space=pltpu.HBM)
+PARTS = 6
+UPDATE = 72
+PART_ROWS = CHUNKS // PARTS * LANES
 
 
 def strain_table():
@@ -119,35 +123,48 @@
     return jnp.where(lane_iota(value.shape[0]) >= 124, 0.0, pltpu.roll(value, LANES - 4, 1))
 
 
-def pack_kernel(state_ref, state_slot_ref, home_slot_ref, disp_ref, out_ref, scratch):
+def part_copy(src, dst, sems, part):
+    rows = pl.ds(part * PART_ROWS, min(PART_ROWS, CASES * ROWS - part * PART_ROWS))
+    return pltpu.make_async_copy(src.at[rows], dst.at[rows], sems.at[part])
+
+
+def split_bf16(value):
+    high = value.astype(jnp.bfloat16)
+    rest = value - high.astype(jnp.float32)
+    middle = rest.astype(jnp.bfloat16)
+    low = (rest - middle.astype(jnp.float32)).astype(jnp.bfloat16)
+    return high, middle, low
+
+
+def turn(choose, block):
+    high, middle, low = (
+        lax.dot_general(
+            choose, part, (((1,), (1,)), ((), ())), preferred_element_type=jnp.float32
+        )
+        for part in split_bf16(block)
+    )
+    return (high + middle) + low
+
+
+def pack_kernel(
+    state_ref, state_slot_ref, home_slot_ref, disp_ref, out_ref, held_ref, scratch, sems
+):
+    for part in range(PARTS):
+        part_copy(state_ref, held_ref, sems, part).start()
     owner = sublane_iota(DEV)
     lane = lane_iota(DEV)
-    chosen = (state_slot_ref[...] >> 7) == owner
-    choose = chosen.astype(jnp.float32)
-    for k in range(CHUNKS):
-        if k < CHUNKS - 1:
-            block = state_ref[k * LANES : (k + 1) * LANES, :]
-        else:
-            block = jnp.concatenate(
-                [
-                    state_ref[k * LANES : k * LANES + TAIL, :],
-                    jnp.zeros((LANES - TAIL, LANES), jnp.float32),
-                ],
-                axis=0,
-            )
-        turned = lax.dot_general(
-            choose,
-            block,
-            (((1,), (1,)), ((), ())),
-            precision=HIGHEST,
-            preferred_element_type=jnp.float32,
-        )
-        if k == CHUNKS - 1:
-            home = (home_slot_ref[...] >> 7) == owner
-            local = jnp.sum(jnp.where(home, lane, 0).astype(jnp.float32), axis=1, keepdims=True)
-            extra = node_row(disp_ref, scratch, TAIL)
-            turned = turned + extra + jnp.where(lane == TAIL + NODES, local, 0.0)
-        out_ref[:, 0, k * LANES : (k + 1) * LANES] = turned
+    choose = ((state_slot_ref[...] >> 7) == owner).astype(jnp.float32).astype(jnp.bfloat16)
+    home = (home_slot_ref[...] >> 7) == owner
+    local = jnp.sum(jnp.where(home, lane, 0).astype(jnp.float32), axis=1, keepdims=True)
+    extra = node_row(disp_ref, scratch, TAIL) + jnp.where(lane == TAIL + NODES, local, 0.0)
+    held_ref[CASES * ROWS :, :] = jnp.zeros((WIDE - CASES * ROWS, LANES), jnp.float32)
+    for part in range(PARTS):
+        part_copy(state_ref, held_ref, sems, part).wait()
+        for k in range(part * CHUNKS // PARTS, (part + 1) * CHUNKS // PARTS):
+            turned = turn(choose, held_ref[k * LANES : (k + 1) * LANES, :])
+            if k == CHUNKS - 1:
+                turned = turned + extra
+            out_ref[:, 0, k * LANES : (k + 1) * LANES] = turned
 
 
 def macro_strain_rows(tail):
@@ -206,16 +223,24 @@
     slot_ref,
     load_ref,
     ret_ref,
+    w_out,
+    p_out,
+    q_out,
+    step_ref,
     w_ref,
     p_ref,
     q_ref,
-    step_ref,
     sig_ref,
     lam_ref,
     mu_ref,
     mu2_ref,
     scratch,
+    sems,
 ):
+    saves = [
+        pltpu.make_async_copy(src, dst, sems.at[k])
+        for k, (src, dst) in enumerate(((w_ref, w_out), (p_ref, p_out), (q_ref, q_out)))
+    ]
     zero = jnp.zeros((8, LANES), jnp.float32)
     phase = phase_ref[...]
     mu = jnp.where(
@@ -239,6 +264,7 @@
             ]
             start = end
         tail = turned
+    saves[0].start()
     macro = macro_strain_rows(tail)
     sub = sublane_iota()
     imposed = [
@@ -325,6 +351,7 @@
 
     mean0, _ = stress_pass(w_ref, imposed, True, False)
     square0 = force_pass(w_ref, lambda div, w: -(div + STAB * w), p_ref)
+    saves[1].start()
     mean1, work1 = stress_pass(p_ref, None, True, True)
     step0 = square0 / (work1 + STAB * square0)
     square1 = force_pass(p_ref, lambda div, p: p - step0 * (div + STAB * p), q_ref)
@@ -342,6 +369,7 @@
         return total
 
     length = lax.fori_loop(0, R, direction, zero)
+    saves[2].start()
     mean2, work2 = stress_pass(q_ref, None, False, True)
     step1 = square1 / (work2 + STAB * length)
     step_ref[0:8, :] = step0
@@ -365,17 +393,16 @@
     for peer in range(DEV):
         ret_ref[8 * peer : 8 * peer + 8, :] = shared
     ret_ref[pl.ds(7, DEV, stride=8), :] = special
+    for save in saves:
+        save.wait()
 
 
 def update_kernel(w_ref, p_ref, q_ref, step_ref, out_ref):
     for case in range(CASES):
         first = step_ref[case : case + 1, :]
         second = step_ref[8 + case : 9 + case, :]
-        for start in range(0, ROWS, 72):
-            rows = pl.ds(start * 8 + case, 72, stride=8)
-            out_ref[case * ROWS + start : case * ROWS + start + 72, :] = (
-                w_ref[rows, :] + first * p_ref[rows, :] + second * q_ref[rows, :]
-            )
+        rows = pl.ds(case, UPDATE, stride=8)
+        out_ref[case] = w_ref[rows, :] + first * p_ref[rows, :] + second * q_ref[rows, :]
 
 
 def row_of(value, index):
@@ -477,18 +504,25 @@
     sent = pl.pallas_call(
         pack_kernel,
         out_shape=jax.ShapeDtypeStruct((DEV, 1, WIDE), f32),
-        in_specs=[VMEM] * 4,
+        in_specs=[HBM] + [VMEM] * 3,
         out_specs=VMEM,
-        scratch_shapes=[pltpu.VMEM((8, LANES), f32)],
+        scratch_shapes=[
+            pltpu.VMEM((WIDE, LANES), f32),
+            pltpu.VMEM((8, LANES), f32),
+            pltpu.SemaphoreType.DMA((PARTS,)),
+        ],
+        compiler_params=pltpu.CompilerParams(vmem_limit_bytes=12 << 20),
         name="pack",
     )(
-        micro_state.reshape(CASES * ROWS, LANES),
+        pltpu.with_memory_space_constraint(
+            micro_state.reshape(CASES * ROWS, LANES), pltpu.HBM
+        ),
         state_slot.reshape(1, LANES),
         home_row,
         displacement,
     )
     received = exchange(sent)
-    big = jax.ShapeDtypeStruct((ROWS * 8, LANES), f32)
+    big = pltpu.HBM((ROWS * 8, LANES), f32)
     answer, w, p, q, steps = pl.pallas_call(
         solve_kernel,
         out_shape=(
@@ -499,22 +533,30 @@
             jax.ShapeDtypeStruct((16, LANES), f32),
         ),
         in_specs=[VMEM, VMEM, SMEM, VMEM, VMEM],
-        out_specs=[VMEM] * 5,
+        out_specs=[VMEM, HBM, HBM, HBM, VMEM],
         scratch_shapes=[
+            pltpu.VMEM((ROWS * 8, LANES), f32),
+            pltpu.VMEM((ROWS * 8, LANES), f32),
+            pltpu.VMEM((ROWS * 8, LANES), f32),
             pltpu.VMEM((6 * VOX * 8, LANES), f32),
             pltpu.VMEM((VOX, LANES), f32),
             pltpu.VMEM((VOX, LANES), f32),
             pltpu.VMEM((VOX, LANES), f32),
             pltpu.VMEM((8, LANES), f32),
+            pltpu.SemaphoreType.DMA((3,)),
         ],
+        compiler_params=pltpu.CompilerParams(vmem_limit_bytes=32 << 20),
         name="solve",
     )(received, phases, phase_moduli, home_row, load)
     returned = exchange(answer.reshape(DEV, 8, LANES)).reshape(DEV * 8, LANES)
     new_state = pl.pallas_call(
         update_kernel,
-        out_shape=jax.ShapeDtypeStruct((CASES * ROWS, LANES), f32),
-        in_specs=[VMEM] * 4,
-        out_specs=VMEM,
+        out_shape=jax.ShapeDtypeStruct((CASES, ROWS, LANES), f32),
+        grid=(ROWS // UPDATE,),
+        in_specs=[pl.BlockSpec((UPDATE * 8, LANES), lambda k: (k, 0))] * 3
+        + [pl.BlockSpec((16, LANES), lambda k: (0, 0))],
+        out_specs=pl.BlockSpec((CASES, UPDATE, LANES), lambda k: (0, k, 0)),
+        compiler_params=pltpu.CompilerParams(vmem_limit_bytes=8 << 20),
         cost_estimate=pl.CostEstimate(
             flops=20_000_000, bytes_accessed=10_000_000, transcendentals=0
         ),
@@ -528,6 +570,7 @@
         in_specs=[VMEM, SMEM, VMEM, VMEM, VMEM, VMEM],
         out_specs=[VMEM] * 3,
         scratch_shapes=[pltpu.VMEM((8, LANES), f32)],
+        compiler_params=pltpu.CompilerParams(vmem_limit_bytes=12 << 20),
         name="final",
     )(
         returned,

time: 88.6 us -> 81.7 us (0.922)
  Pallas kernels: 30.4 us -> 20.1 us
  local copies, waits for them, and re-layouts: 0.8 us -> 7.27 us
  waiting for transfers between devices: 7.56 us -> 4.58 us
    unnamed x2 -> x28, local copies, waits for them, and re-layouts: 0.8 us -> 7.27 us
    pallas_call x1, Pallas kernels: 7.96 us -> 4.67 us  [per_device(): pl.pallas_call(pack_kernel, out_shape=jax.ShapeDtypeStruct((DEV, 1, WIDE)...]
    pallas_call x1, Pallas kernels: 12.8 us -> 9.49 us  [per_device(): pl.pallas_call(solve_kernel, out_shape=(jax.ShapeDtypeStruct((DEV * 8, LA...]
    all_to_all x1, waiting for transfers between devices: 7.56 us -> 4.58 us  [exchange(): return lax.all_to_all(value, AXES, split_axis=0, concat_axis=0, tiled=True)]
    pallas_call x1, Pallas kernels: 6.48 us -> 4.2 us  [per_device(): pl.pallas_call(update_kernel, out_shape=jax.ShapeDtypeStruct((CASES, ROWS...]
    pallas_call x1, Pallas kernels: 3.18 us -> 1.8 us  [per_device(): pl.pallas_call(final_kernel, out_shape=(node_shape, node_shape, jax.Shape...]
  transfers between devices with their start and end apart: 1 -> 1, of which waited for: 1 -> 1; matrix products, arithmetic and copies ran while one was open for 0% -> 0% of each run, Pallas kernels for 7% -> 5%
where the time goes in v1:
time: 81.7 us; the launch traced here: 81.4 us
  blocking collectives  44.9 us (55%)
  Pallas kernels  20.1 us (25%)
  local copies, waits for them, and re-layouts  7.27 us (9%)
  waiting for transfers between devices  4.58 us (6%)
  starting transfers between devices  3.76 us (5%)
    all_to_all x1, blocking collectives, exchange(): return lax.all_to_all(value, AXES, split_axis=0, concat_axis=0, tiled=True)  44.9 us
    pallas_call x1, Pallas kernels, per_device(): pl.pallas_call(solve_kernel, out_shape=(jax.ShapeDtypeStruct((DEV * 8, LA...  9.49 us
    unnamed x28, local copies, waits for them, and re-layouts  7.27 us
    pallas_call x1, Pallas kernels, per_device(): pl.pallas_call(pack_kernel, out_shape=jax.ShapeDtypeStruct((DEV, 1, WIDE)...  4.67 us
    all_to_all x1, waiting for transfers between devices, exchange(): return lax.all_to_all(value, AXES, split_axis=0, concat_axis=0, tiled=True)  4.58 us
    pallas_call x1, Pallas kernels, per_device(): pl.pallas_call(update_kernel, out_shape=jax.ShapeDtypeStruct((CASES, ROWS...  4.2 us
    all_to_all x1, starting transfers between devices, exchange(): return lax.all_to_all(value, AXES, split_axis=0, concat_axis=0, tiled=True)  3.76 us
    pallas_call x1, Pallas kernels, per_device(): pl.pallas_call(final_kernel, out_shape=(node_shape, node_shape, jax.Shape...  1.8 us
  transfers between devices with their start and end apart: 1, of which 1 were waited for; matrix products, arithmetic and copies ran while one was open for 0% of the time, Pallas kernels for 5%

profile of v1, /device:TPU:1, one launch (start us, length us, event | category | flops | bytes accessed | tf_op | source)
XLA Modules:
  0.0 81.4 jit_solution(17005129770460121630)
XLA Ops:
  0.6 0.0 copy-start.7
  0.6 0.7 copy-done.7
  1.3 0.0 copy-start.10
  1.3 0.7 copy-done.10
  2.0 0.0 copy-start.13
  2.0 0.7 copy-done.13
  2.6 4.7 %pack.1 = f32[128,1,4608]{2,1,0:T(1,128)S(1)} custom-call(f32[4536,128]{1,0:T(8,128)} %bitcast.13, s32[1,128]{1,0:T(1,128)S(1)} %bitcast.11, s32[1,128]{1,0:T(1,128)S(1)} %bitcast.9, f32[3,1,2,8]{3,2,1,0:T(2,128)S(1)} %copy-done.7), custom_call_target="tpu_custom_call" | custom-call | tf_op jit(solution)/shard_map/pack/pallas_call | solution.py:504
  7.3 0.0 copy-start.5
  7.3 0.0 copy-start.9
  7.3 0.0 copy-start.11
  7.3 0.0 copy-start.12
  7.4 44.9 %all_to_all.10.recv_ref = f32[128,1,4608]{2,1,0:T(1,128)S(1)} all-to-all(f32[128,1,4608]{2,1,0:T(1,128)S(1)} %pack.1), channel_id=1, replica_groups=mesh['sub'=32,'rve'=4] {'sub','rve'}, dimensions={0} | all-to-all | bytes 4718592 | tf_op jit(solution)/shard_map/all_to_all | solution.py:497
  52.2 0.0 copy-done.5
  52.2 0.0 copy-done.9
  52.2 0.0 copy-done.11
  52.2 0.0 copy-done.12
  52.2 9.5 %solve.1 = (f32[1024,128]{1,0:T(8,128)}, f32[5184,128]{1,0:T(8,128)}, f32[5184,128]{1,0:T(8,128)}, f32[5184,128]{1,0:T(8,128)}, f32[16,128]{1,0:T(8,128)S(1)}) custom-call(f32[128,1,4608]{2,1,0:T(1,128)S(1)} %all_to_all.10.recv_ref, s32[216,128]{1,0:T(8,128)S(1)} %copy-done.5, f32[2,3]{1,0:T(2,128)S(1)} %copy-done.12, s32[1,128]{1,0:T(1,128)S(1)} %bitcast.10, ...), custom_call_target="tpu_custom_call" | custom-call | tf_op jit(solution)/shard_map/solve/pallas_call | solution.py:526
  61.7 3.8 %all-to-all-start.1 = ((f32[128,8,128]{2,1,0:T(8,128)}), f32[128,8,128]{2,1,0:T(8,128)S(1)}, u32[]{:S(2)}, u32[]{:S(2)}) async-start(f32[128,8,128]{2,1,0:T(8,128)} %bitcast.4), calls=%async_computation.1 | async-start | bytes 1048576 | tf_op jit(solution)/shard_map/all_to_all | solution.py:497
  65.5 0.0 copy-start
  65.5 1.7 %copy-done = f32[5184,128]{1,0:T(8,128)S(1)} copy-done((f32[5184,128]{1,0:T(8,128)S(1)}, f32[5184,128]{1,0:T(8,128)}, u32[]{:S(2)}) %copy-start) | copy-done | bytes 2654232
  67.3 0.0 copy-start.1
  67.3 1.7 %copy-done.1 = f32[5184,128]{1,0:T(8,128)S(1)} copy-done((f32[5184,128]{1,0:T(8,128)S(1)}, f32[5184,128]{1,0:T(8,128)}, u32[]{:S(2)}) %copy-start.1) | copy-done | bytes 2654232
  69.0 0.0 copy-start.2
  69.0 1.7 %copy-done.2 = f32[5184,128]{1,0:T(8,128)S(1)} copy-done((f32[5184,128]{1,0:T(8,128)S(1)}, f32[5184,128]{1,0:T(8,128)}, u32[]{:S(2)}) %copy-start.2) | copy-done | bytes 2654232
  70.8 0.0 copy-start.3
  70.8 0.0 copy-start.4
  70.8 0.0 copy-start.6
  70.8 0.0 copy-start.8
  70.8 4.2 %update.1 = f32[7,648,128]{2,1,0:T(8,128)} custom-call(f32[5184,128]{1,0:T(8,128)S(1)} %copy-done, f32[5184,128]{1,0:T(8,128)S(1)} %copy-done.1, f32[5184,128]{1,0:T(8,128)S(1)} %copy-done.2, f32[16,128]{1,0:T(8,128)S(1)} %get-tuple-element.15.step_ref), custom_call_target="tpu_custom_call" | custom-call | flops 20000000 | bytes 10000000 | tf_op jit(solution)/shard_map/update/pallas_call | solution.py:552
  75.0 4.6 %all-to-all-done.1 = f32[128,8,128]{2,1,0:T(8,128)S(1)} async-done(((f32[128,8,128]{2,1,0:T(8,128)}), f32[128,8,128]{2,1,0:T(8,128)S(1)}, u32[]{:S(2)}, u32[]{:S(2)}) %all-to-all-start.1) | async-done | bytes 524320 | tf_op jit(solution)/shard_map/all_to_all | solution.py:497
  79.6 0.0 copy-done.3
  79.6 0.0 copy-done.4
  79.6 0.0 copy-done.6
  79.6 0.0 copy-done.8
  79.6 1.8 %final.1 = (f32[3,1,2,8]{3,2,1,0:T(2,128)}, f32[3,1,2,8]{3,2,1,0:T(2,128)}, f32[1,1]{1,0:T(1,128)}) custom-call(f32[1024,128]{1,0:T(8,128)S(1)} %bitcast.8, s32[1,1]{1,0:T(1,128)} %bitcast.6.me_ref, f32[3,1,2,8]{3,2,1,0:T(2,128)S(1)} %copy-done.8, f32[768,256]{1,0:T(8,128)S(1)} %copy-done.3, f32[144,128]{1,0:T(8,128)S(1)} %copy-done.6, ...), custom_call_target="tpu_custom_call" | custom-call | tf_op jit(solution)/shard_map/final/pallas_call | solution.py:567
Async XLA Ops:
  0.6 0.7 copy-start.7
  1.3 0.7 copy-start.10
  2.0 0.7 copy-start.13
  7.3 44.9 %copy-start.5 = (s32[216,128]{1,0:T(8,128)S(1)}, s32[216,128]{1,0:T(8,128)}, u32[]{:S(2)}) copy-start(s32[216,128]{1,0:T(8,128)} %phase_ref.1) | copy-start | bytes 331780
  7.3 44.9 %copy-start.9 = (f32[3,1,2,8]{3,2,1,0:T(2,128)S(1)}, f32[3,1,2,8]{3,2,1,0:T(2,128)}, u32[]{:S(2)}) copy-start(f32[3,1,2,8]{3,2,1,0:T(2,128)} %load_ref.1) | copy-start | bytes 580
  7.3 44.9 %copy-start.11 = (s32[128]{0:T(128)S(1)}, s32[128]{0:T(128)}, u32[]{:S(2)}) copy-start(s32[128]{0:T(128)} %param.12) | copy-start | bytes 1540
  7.3 44.9 %copy-start.12 = (f32[2,3]{1,0:T(2,128)S(1)}, f32[2,3]{1,0:T(2,128)}, u32[]{:S(2)}) copy-start(f32[2,3]{1,0:T(2,128)} %moduli_ref.1) | copy-start | bytes 76
  61.7 17.8 %all-to-all-start.1 = ((f32[128,8,128]{2,1,0:T(8,128)}), f32[128,8,128]{2,1,0:T(8,128)S(1)}, u32[]{:S(2)}, u32[]{:S(2)}) async-start(f32[128,8,128]{2,1,0:T(8,128)} %bitcast.4), calls=%async_computation.1 | async-start | bytes 1048576 | tf_op jit(solution)/shard_map/all_to_all | solution.py:497
  65.5 1.8 %copy-start = (f32[5184,128]{1,0:T(8,128)S(1)}, f32[5184,128]{1,0:T(8,128)}, u32[]{:S(2)}) copy-start(f32[5184,128]{1,0:T(8,128)} %get-tuple-element.12.w_ref) | copy-start | bytes 7962628
  67.3 1.7 %copy-start.1 = (f32[5184,128]{1,0:T(8,128)S(1)}, f32[5184,128]{1,0:T(8,128)}, u32[]{:S(2)}) copy-start(f32[5184,128]{1,0:T(8,128)} %get-tuple-element.13.p_ref) | copy-start | bytes 7962628
  69.0 1.7 %copy-start.2 = (f32[5184,128]{1,0:T(8,128)S(1)}, f32[5184,128]{1,0:T(8,128)}, u32[]{:S(2)}) copy-start(f32[5184,128]{1,0:T(8,128)} %get-tuple-element.14.q_ref) | copy-start | bytes 7962628
  70.8 8.8 %copy-start.3 = (f32[768,256]{1,0:T(8,128)S(1)}, f32[768,256]{1,0:T(8,128)}, u32[]{:S(2)}) copy-start(f32[768,256]{1,0:T(8,128)} %constant.17.clone.force_ref) | copy-start | bytes 2359300
  70.8 8.8 %copy-start.4 = (f32[4,128,128]{2,1,0:T(8,128)S(1)}, f32[4,128,128]{2,1,0:T(8,128)}, u32[]{:S(2)}) copy-start(f32[4,128,128]{2,1,0:T(8,128)} %constant.19.clone.place_ref) | copy-start | bytes 786436
  70.8 8.8 %copy-start.6 = (f32[144,128]{1,0:T(8,128)S(1)}, f32[144,128]{1,0:T(8,128)}, u32[]{:S(2)}) copy-start(f32[144,128]{1,0:T(8,128)} %constant.18.clone.weight_ref) | copy-start | bytes 221188
  70.8 8.8 %copy-start.8 = (f32[3,1,2,8]{3,2,1,0:T(2,128)S(1)}, f32[3,1,2,8]{3,2,1,0:T(2,128)}, u32[]{:S(2)}) copy-start(f32[3,1,2,8]{3,2,1,0:T(2,128)} %disp_ref.3) | copy-start | bytes 580

commit v2 on v1

--- a/solution.py
+++ b/solution.py
@@ -6,6 +6,7 @@
 from jax import lax
 from jax.experimental import pallas as pl
 from jax.experimental.pallas import tpu as pltpu
+from jax.sharding import Mesh
 from jax.sharding import PartitionSpec as P
 
 R = 6
@@ -20,7 +21,9 @@
 NODES = 48
 STAB = 0.1
 FLOOR = 1.0
-AXES = ("sub", "rve")
+SPLIT = ("far", "core", "rve")
+AXES = ("core", "far", "rve")
+SUB = ("far", "core")
 PAIRS = ((0, 5, 4), (5, 1, 3), (4, 3, 2))
 STRAIN_OF = ((0, 4, 5), (5, 1, 3), (4, 3, 2))
 OFF_DIAGONAL = ((0, 4), (0, 5), (4, 5), (1, 3), (1, 5), (3, 5), (2, 3), (2, 4), (3, 4))
@@ -116,11 +119,23 @@
 
 
 def below_lanes(value):
-    return jnp.where(lane_iota(value.shape[0]) < 4, 0.0, pltpu.roll(value, 4, 1))
+    lane = lane_iota(value.shape[0])
+    moved = jnp.where(lane < 64, pltpu.roll(value, 68, 1), pltpu.roll(value, 64, 1))
+    return jnp.where(lane < 4, 0.0, moved)
 
 
 def above_lanes(value):
-    return jnp.where(lane_iota(value.shape[0]) >= 124, 0.0, pltpu.roll(value, LANES - 4, 1))
+    lane = lane_iota(value.shape[0])
+    moved = jnp.where(lane < 64, pltpu.roll(value, 64, 1), pltpu.roll(value, 60, 1))
+    return jnp.where(lane >= 124, 0.0, moved)
+
+
+def device_at(place):
+    return ((place >> 2) & 15) * 8 + (place >> 6) * 4 + (place & 3)
+
+
+def place_of(device):
+    return ((device >> 2) & 1) * 64 + (device >> 3) * 4 + (device & 3)
 
 
 def part_copy(src, dst, sems, part):
@@ -147,12 +162,36 @@
 
 
 def pack_kernel(
-    state_ref, state_slot_ref, home_slot_ref, disp_ref, out_ref, held_ref, scratch, sems
+    state_ref,
+    state_slot_hbm,
+    home_slot_hbm,
+    disp_hbm,
+    out_ref,
+    held_ref,
+    state_slot_ref,
+    home_slot_ref,
+    disp_ref,
+    scratch,
+    sems,
 ):
+    small = [
+        pltpu.make_async_copy(src, dst, sems.at[PARTS + k])
+        for k, (src, dst) in enumerate(
+            (
+                (state_slot_hbm, state_slot_ref),
+                (home_slot_hbm, home_slot_ref),
+                (disp_hbm, disp_ref),
+            )
+        )
+    ]
+    for copy in small:
+        copy.start()
     for part in range(PARTS):
         part_copy(state_ref, held_ref, sems, part).start()
-    owner = sublane_iota(DEV)
+    owner = device_at(sublane_iota(DEV))
     lane = lane_iota(DEV)
+    for copy in small:
+        copy.wait()
     choose = ((state_slot_ref[...] >> 7) == owner).astype(jnp.float32).astype(jnp.bfloat16)
     home = (home_slot_ref[...] >> 7) == owner
     local = jnp.sum(jnp.where(home, lane, 0).astype(jnp.float32), axis=1, keepdims=True)
@@ -164,7 +203,7 @@
             turned = turn(choose, held_ref[k * LANES : (k + 1) * LANES, :])
             if k == CHUNKS - 1:
                 turned = turned + extra
-            out_ref[:, 0, k * LANES : (k + 1) * LANES] = turned
+            out_ref[pl.ds(k, DEV, stride=CHUNKS), :] = turned
 
 
 def macro_strain_rows(tail):
@@ -241,8 +280,14 @@
         pltpu.make_async_copy(src, dst, sems.at[k])
         for k, (src, dst) in enumerate(((w_ref, w_out), (p_ref, p_out), (q_ref, q_out)))
     ]
+
+    def save_plane(base):
+        for i in range(3):
+            rows = pl.ds(base + i * VOX * 8, 288)
+            pltpu.make_async_copy(q_ref.at[rows], q_out.at[rows], sems.at[2]).start()
+
     zero = jnp.zeros((8, LANES), jnp.float32)
-    phase = phase_ref[...]
+    phase = jnp.take_along_axis(phase_ref[...], device_at(lane_iota(VOX)), axis=1)
     mu = jnp.where(
         phase == 0, moduli_ref[1, 0], jnp.where(phase == 1, moduli_ref[1, 1], moduli_ref[1, 2])
     )
@@ -254,7 +299,7 @@
     w_ref[pl.ds(7, ROWS, stride=8), :] = jnp.zeros((ROWS, LANES), jnp.float32)
     tail = None
     for k in range(CHUNKS):
-        turned = recv_ref[:, 0, k * LANES : (k + 1) * LANES].T
+        turned = recv_ref[pl.ds(k, DEV, stride=CHUNKS), :].T
         start, stop = k * LANES, min((k + 1) * LANES, CASES * ROWS)
         while start < stop:
             case = start // ROWS
@@ -326,7 +371,8 @@
         return lax.fori_loop(0, R, plane, ((zero,) * 6, zero))
 
     def force_pass(src, finish, dst):
-        def plane(a, total):
+        def plane(a, carry):
+            totals = list(carry)
             base = pl.multiple_of(a * 288, 8)
             behind = pl.multiple_of(jnp.where(a == 0, (R - 1) * 288, (a - 1) * 288), 8)
             for b in range(R):
@@ -343,11 +389,12 @@
                         ) + last[i]
                         value = finish(come - gone, tile_at(src, base, i * VOX + at))
                         dst[pl.ds(base + (i * VOX + at) * 8, 8), :] = value
-                        total = total + value * value
+                        totals[i] = totals[i] + value * value
                     last = [own[PAIRS[2][i]] for i in range(3)]
-            return total
-
-        return lax.fori_loop(0, R, plane, zero)
+            return tuple(totals)
+
+        totals = lax.fori_loop(0, R, plane, (zero,) * 3)
+        return (totals[0] + totals[1]) + totals[2]
 
     mean0, _ = stress_pass(w_ref, imposed, True, False)
     square0 = force_pass(w_ref, lambda div, w: -(div + STAB * w), p_ref)
@@ -357,26 +404,28 @@
     square1 = force_pass(p_ref, lambda div, p: p - step0 * (div + STAB * p), q_ref)
     ratio = square1 / square0
 
-    def direction(a, total):
+    def direction(a, carry):
+        totals = list(carry)
         base = pl.multiple_of(a * 288, 8)
-        for i in range(3):
-            for at in range(36):
+        for at in range(36):
+            for i in range(3):
                 value = tile_at(q_ref, base, i * VOX + at) + ratio * tile_at(
                     p_ref, base, i * VOX + at
                 )
                 q_ref[pl.ds(base + (i * VOX + at) * 8, 8), :] = value
-                total = total + value * value
-        return total
-
-    length = lax.fori_loop(0, R, direction, zero)
-    saves[2].start()
+                totals[i] = totals[i] + value * value
+        save_plane(base)
+        return tuple(totals)
+
+    totals = lax.fori_loop(0, R, direction, (zero,) * 3)
+    length = (totals[0] + totals[1]) + totals[2]
     mean2, work2 = stress_pass(q_ref, None, False, True)
     step1 = square1 / (work2 + STAB * length)
     step_ref[0:8, :] = step0
     step_ref[8:16, :] = step1
     mean = [(mean0[m] + step0 * mean1[m] + step1 * mean2[m]) * (1.0 / VOX) for m in range(6)]
 
-    shared = (slot_ref[...] >> 7).astype(jnp.float32)
+    shared = place_of(slot_ref[...] >> 7).astype(jnp.float32)
     shared = jnp.broadcast_to(shared, (8, LANES))
     for m in range(6):
         shared = jnp.where(sub == m, mean[m][0:1], shared)
@@ -398,11 +447,13 @@
 
 
 def update_kernel(w_ref, p_ref, q_ref, step_ref, out_ref):
+    place = place_of(lane_iota(UPDATE))
     for case in range(CASES):
         first = step_ref[case : case + 1, :]
         second = step_ref[8 + case : 9 + case, :]
         rows = pl.ds(case, UPDATE, stride=8)
-        out_ref[case] = w_ref[rows, :] + first * p_ref[rows, :] + second * q_ref[rows, :]
+        value = w_ref[rows, :] + first * p_ref[rows, :] + second * q_ref[rows, :]
+        out_ref[case] = jnp.take_along_axis(value, place, axis=1)
 
 
 def row_of(value, index):
@@ -445,7 +496,9 @@
         preferred_element_type=jnp.float32,
     )
     home = sublane_iota(DEV)
-    lifted = jnp.where(home < 4, 0.0, pltpu.roll(forces[:, LANES:], 4, 0))
+    upper = forces[:, LANES:]
+    lifted = jnp.where(home < 64, pltpu.roll(upper, 68, 0), pltpu.roll(upper, 64, 0))
+    lifted = jnp.where(home < 4, 0.0, lifted)
     near = forces[:, :LANES] + lifted
     beside = jnp.where(home % 4 == 0, pltpu.roll(near, DEV - 3, 0), pltpu.roll(near, 1, 0))
     force = near + pltpu.roll(beside, LANES - NODES, 1)
@@ -458,7 +511,7 @@
 
     own_residual = row_of(residual, me)
     left = jnp.where(me % 4 == 0, me + 3, me - 1)
-    under = jnp.where(me < 4, 0, 4)
+    under = jnp.where(me >= 64, 64, jnp.where(me < 4, 0, -60))
     turned = special.T
     diagonal = jnp.zeros((24, LANES), jnp.float32)
     for k, source in enumerate((me, left, me - under, left - under)):
@@ -493,6 +546,10 @@
             ref[i, 0] = tile[2 * i : 2 * i + 2, 0:8]
 
 
+def in_hbm(value):
+    return pltpu.with_memory_space_constraint(value, pltpu.HBM)
+
+
 def exchange(value):
     return lax.all_to_all(value, AXES, split_axis=0, concat_axis=0, tiled=True)
 
@@ -503,25 +560,26 @@
     home_row = home_slot.reshape(1, LANES)
     sent = pl.pallas_call(
         pack_kernel,
-        out_shape=jax.ShapeDtypeStruct((DEV, 1, WIDE), f32),
-        in_specs=[HBM] + [VMEM] * 3,
+        out_shape=jax.ShapeDtypeStruct((DEV * CHUNKS, LANES), f32),
+        in_specs=[HBM] * 4,
         out_specs=VMEM,
         scratch_shapes=[
             pltpu.VMEM((WIDE, LANES), f32),
+            pltpu.VMEM((1, LANES), jnp.int32),
+            pltpu.VMEM((1, LANES), jnp.int32),
+            pltpu.VMEM(displacement.shape, f32),
             pltpu.VMEM((8, LANES), f32),
-            pltpu.SemaphoreType.DMA((PARTS,)),
+            pltpu.SemaphoreType.DMA((PARTS + 3,)),
         ],
         compiler_params=pltpu.CompilerParams(vmem_limit_bytes=12 << 20),
         name="pack",
     )(
-        pltpu.with_memory_space_constraint(
-            micro_state.reshape(CASES * ROWS, LANES), pltpu.HBM
-        ),
-        state_slot.reshape(1, LANES),
-        home_row,
-        displacement,
-    )
-    received = exchange(sent)
+        in_hbm(micro_state.reshape(CASES * ROWS, LANES)),
+        in_hbm(state_slot.reshape(1, LANES)),
+        in_hbm(home_row),
+        in_hbm(displacement),
+    )
+    received = exchange(sent.reshape(DEV, 1, WIDE)).reshape(DEV * CHUNKS, LANES)
     big = pltpu.HBM((ROWS * 8, LANES), f32)
     answer, w, p, q, steps = pl.pallas_call(
         solve_kernel,
@@ -561,7 +619,7 @@
             flops=20_000_000, bytes_accessed=10_000_000, transcendentals=0
         ),
         name="update",
-    )(w, p, q, steps)
+    )(in_hbm(w), in_hbm(p), in_hbm(q), steps)
     me = lax.axis_index(AXES).astype(jnp.int32).reshape(1, 1)
     node_shape = jax.ShapeDtypeStruct(displacement.shape, f32)
     displaced, residual, rel_norm = pl.pallas_call(
@@ -589,22 +647,23 @@
 
 
 def solution(mesh):
+    split = Mesh(mesh.devices.reshape(-1, 2, mesh.shape["rve"]), SPLIT)
     return jax.shard_map(
         per_device,
-        mesh=mesh,
+        mesh=split,
         in_specs=(
-            P(None, "sub", "rve", None),
-            P(None, "sub", "rve", None),
-            P(AXES),
-            P(None, None, None, AXES),
-            P(AXES),
-            P(None, AXES),
+            P(None, SUB, "rve", None),
+            P(None, SUB, "rve", None),
+            P(SPLIT),
+            P(None, None, None, SPLIT),
+            P(SPLIT),
+            P(None, SPLIT),
             P(),
         ),
         out_specs=(
-            P(None, None, None, AXES),
-            P(None, "sub", "rve", None),
-            P(None, "sub", "rve", None),
+            P(None, None, None, SPLIT),
+            P(None, SUB, "rve", None),
+            P(None, SUB, "rve", None),
             P(),
         ),
         check_vma=False,

time: 81.7 us -> 78.7 us (0.963)
  local copies, waits for them, and re-layouts: 7.27 us -> 0.05 us
  Pallas kernels: 20.1 us -> 23.4 us
  starting transfers between devices: 3.76 us -> 6.32 us
  blocking collectives: 44.9 us -> 42.6 us
    unnamed x28 -> x16, local copies, waits for them, and re-layouts: 7.27 us -> 0.05 us
    pallas_call x1, Pallas kernels: 4.2 us -> 8.18 us  [per_device(): pl.pallas_call(update_kernel, out_shape=jax.ShapeDtypeStruct((CASES, ROWS...]
    all_to_all x1, starting transfers between devices: 3.76 us -> 6.32 us  [exchange(): return lax.all_to_all(value, AXES, split_axis=0, concat_axis=0, tiled=True)]
    all_to_all x1, blocking collectives: 44.9 us -> 42.6 us  [exchange(): return lax.all_to_all(value, AXES, split_axis=0, concat_axis=0, tiled=True)]
  transfers between devices with their start and end apart: 1 -> 1, of which waited for: 1 -> 1; matrix products, arithmetic and copies ran while one was open for 0% -> 0% of each run, Pallas kernels for 5% -> 10%
where the time goes in v2:
time: 78.7 us; the launch traced here: 78.4 us
  blocking collectives  42.6 us (54%)
  Pallas kernels  23.4 us (30%)
  starting transfers between devices  6.32 us (8%)
  waiting for transfers between devices  5.25 us (7%)
    all_to_all x1, blocking collectives, exchange(): return lax.all_to_all(value, AXES, split_axis=0, concat_axis=0, tiled=True)  42.6 us
    pallas_call x1, Pallas kernels, per_device(): pl.pallas_call(solve_kernel, out_shape=(jax.ShapeDtypeStruct((DEV * 8, LA...  9.1 us
    pallas_call x1, Pallas kernels, per_device(): pl.pallas_call(update_kernel, out_shape=jax.ShapeDtypeStruct((CASES, ROWS...  8.18 us
    all_to_all x1, starting transfers between devices, exchange(): return lax.all_to_all(value, AXES, split_axis=0, concat_axis=0, tiled=True)  6.32 us
    all_to_all x1, waiting for transfers between devices, exchange(): return lax.all_to_all(value, AXES, split_axis=0, concat_axis=0, tiled=True)  5.25 us
    pallas_call x1, Pallas kernels, per_device(): pl.pallas_call(pack_kernel, out_shape=jax.ShapeDtypeStruct((DEV * CHUNKS,...  4.31 us
    pallas_call x1, Pallas kernels, per_device(): pl.pallas_call(final_kernel, out_shape=(node_shape, node_shape, jax.Shape...  1.79 us
  transfers between devices with their start and end apart: 1, of which 1 were waited for; matrix products, arithmetic and copies ran while one was open for 0% of the time, Pallas kernels for 10%

profile of v2, /device:TPU:1, one launch (start us, length us, event | category | flops | bytes accessed | tf_op | source)
XLA Modules:
  0.0 78.4 jit_solution(11592078857376652581)
XLA Ops:
  0.6 4.3 %pack.1 = f32[4608,128]{1,0:T(8,128)S(1)} custom-call(f32[4536,128]{1,0:T(8,128)} %bitcast.16, s32[1,128]{1,0:T(1,128)} %bitcast.17, s32[1,128]{1,0:T(1,128)} %bitcast.13, f32[3,1,2,8]{3,2,1,0:T(2,128)} %disp_ref.1), custom_call_target="tpu_custom_call" | custom-call | tf_op jit(solution)/shard_map/pack/pallas_call | solution.py:561
  4.9 0.0 copy-start.2
  5.0 0.0 copy-start.5
  5.0 0.0 copy-start.6
  5.0 0.0 copy-start.7
  5.0 42.6 %all_to_all.10 = f32[128,1,4608]{2,1,0:T(1,128)S(1)} all-to-all(f32[128,1,4608]{2,1,0:T(1,128)S(1)} %bitcast.11), channel_id=1, replica_groups=mesh['far'=16,'core'=2,'rve'=4] {'core','far','rve'}, dimensions={0} | all-to-all | bytes 4718592 | tf_op jit(solution)/shard_map/all_to_all | solution.py:554
  47.6 0.0 copy-done.2
  47.6 0.0 copy-done.5
  47.6 0.0 copy-done.6
  47.6 0.0 copy-done.7
  47.6 9.1 %solve.1 = (f32[1024,128]{1,0:T(8,128)}, f32[5184,128]{1,0:T(8,128)}, f32[5184,128]{1,0:T(8,128)}, f32[5184,128]{1,0:T(8,128)}, f32[16,128]{1,0:T(8,128)S(1)}) custom-call(f32[4608,128]{1,0:T(8,128)S(1)} %bitcast.10, s32[216,128]{1,0:T(8,128)S(1)} %copy-done.2, f32[2,3]{1,0:T(2,128)S(1)} %copy-done.7, s32[1,128]{1,0:T(1,128)S(1)} %bitcast.14, ...), custom_call_target="tpu_custom_call" | custom-call | tf_op jit(solution)/shard_map/solve/pallas_call | solution.py:584
  56.7 6.3 %all-to-all-start.1 = ((f32[128,8,128]{2,1,0:T(8,128)}), f32[128,8,128]{2,1,0:T(8,128)S(1)}, u32[]{:S(2)}, u32[]{:S(2)}) async-start(f32[128,8,128]{2,1,0:T(8,128)} %bitcast.6), calls=%async_computation.1 | async-start | bytes 1048576 | tf_op jit(solution)/shard_map/all_to_all | solution.py:554
  63.1 0.0 copy-start
  63.1 0.0 copy-start.1
  63.1 0.0 copy-start.3
  63.1 0.0 copy-start.4
  63.1 8.2 %update.1 = f32[7,648,128]{2,1,0:T(8,128)} custom-call(f32[5184,128]{1,0:T(8,128)} %get-tuple-element.12.w_ref, f32[5184,128]{1,0:T(8,128)} %get-tuple-element.13.p_ref, f32[5184,128]{1,0:T(8,128)} %get-tuple-element.14.q_ref, f32[16,128]{1,0:T(8,128)S(1)} %get-tuple-element.15.step_ref), custom_call_target="tpu_custom_call" | custom-call | flops 20000000 | bytes 10000000 | tf_op jit(solution)/shard_map/update/pallas_call | solution.py:610
  71.3 5.3 %all-to-all-done.1 = f32[128,8,128]{2,1,0:T(8,128)S(1)} async-done(((f32[128,8,128]{2,1,0:T(8,128)}), f32[128,8,128]{2,1,0:T(8,128)S(1)}, u32[]{:S(2)}, u32[]{:S(2)}) %all-to-all-start.1) | async-done | bytes 524320 | tf_op jit(solution)/shard_map/all_to_all | solution.py:554
  76.5 0.0 copy-done
  76.5 0.0 copy-done.1
  76.5 0.0 copy-done.3
  76.6 0.0 copy-done.4
  76.6 1.8 %final.1 = (f32[3,1,2,8]{3,2,1,0:T(2,128)}, f32[3,1,2,8]{3,2,1,0:T(2,128)}, f32[1,1]{1,0:T(1,128)}) custom-call(f32[1024,128]{1,0:T(8,128)S(1)} %bitcast.12, s32[1,1]{1,0:T(1,128)} %bitcast.8.me_ref, f32[3,1,2,8]{3,2,1,0:T(2,128)S(1)} %copy-done.4, f32[768,256]{1,0:T(8,128)S(1)} %copy-done, f32[144,128]{1,0:T(8,128)S(1)} %copy-done.3, ...), custom_call_target="tpu_custom_call" | custom-call | tf_op jit(solution)/shard_map/final/pallas_call | solution.py:625
Async XLA Ops:
  4.9 42.6 %copy-start.2 = (s32[216,128]{1,0:T(8,128)S(1)}, s32[216,128]{1,0:T(8,128)}, u32[]{:S(2)}) copy-start(s32[216,128]{1,0:T(8,128)} %phase_ref.1) | copy-start | bytes 331780
  5.0 42.6 %copy-start.5 = (f32[3,1,2,8]{3,2,1,0:T(2,128)S(1)}, f32[3,1,2,8]{3,2,1,0:T(2,128)}, u32[]{:S(2)}) copy-start(f32[3,1,2,8]{3,2,1,0:T(2,128)} %load_ref.1) | copy-start | bytes 580
  5.0 42.6 %copy-start.6 = (s32[128]{0:T(128)S(1)}, s32[128]{0:T(128)}, u32[]{:S(2)}) copy-start(s32[128]{0:T(128)} %param.12) | copy-start | bytes 1540
  5.0 42.6 %copy-start.7 = (f32[2,3]{1,0:T(2,128)S(1)}, f32[2,3]{1,0:T(2,128)}, u32[]{:S(2)}) copy-start(f32[2,3]{1,0:T(2,128)} %moduli_ref.1) | copy-start | bytes 76
  56.7 19.8 %all-to-all-start.1 = ((f32[128,8,128]{2,1,0:T(8,128)}), f32[128,8,128]{2,1,0:T(8,128)S(1)}, u32[]{:S(2)}, u32[]{:S(2)}) async-start(f32[128,8,128]{2,1,0:T(8,128)} %bitcast.6), calls=%async_computation.1 | async-start | bytes 1048576 | tf_op jit(solution)/shard_map/all_to_all | solution.py:554
  63.1 13.5 %copy-start = (f32[768,256]{1,0:T(8,128)S(1)}, f32[768,256]{1,0:T(8,128)}, u32[]{:S(2)}) copy-start(f32[768,256]{1,0:T(8,128)} %constant.24.clone.force_ref) | copy-start | bytes 2359300
  63.1 13.5 %copy-start.1 = (f32[4,128,128]{2,1,0:T(8,128)S(1)}, f32[4,128,128]{2,1,0:T(8,128)}, u32[]{:S(2)}) copy-start(f32[4,128,128]{2,1,0:T(8,128)} %constant.26.clone.place_ref) | copy-start | bytes 786436
  63.1 13.5 %copy-start.3 = (f32[144,128]{1,0:T(8,128)S(1)}, f32[144,128]{1,0:T(8,128)}, u32[]{:S(2)}) copy-start(f32[144,128]{1,0:T(8,128)} %constant.25.clone.weight_ref) | copy-start | bytes 221188
  63.1 13.5 %copy-start.4 = (f32[3,1,2,8]{3,2,1,0:T(2,128)S(1)}, f32[3,1,2,8]{3,2,1,0:T(2,128)}, u32[]{:S(2)}) copy-start(f32[3,1,2,8]{3,2,1,0:T(2,128)} %disp_ref.1) | copy-start | bytes 580

commit v3 on v2

--- a/solution.py
+++ b/solution.py
@@ -33,9 +33,10 @@
 VMEM = pl.BlockSpec(memory_space=pltpu.VMEM)
 SMEM = pl.BlockSpec(memory_space=pltpu.SMEM)
 HBM = pl.BlockSpec(memory_space=pltpu.HBM)
-PARTS = 6
+CUTS = (0, 18, 30, 36)
+PARTS = len(CUTS) - 1
+STEP = 6
 UPDATE = 72
-PART_ROWS = CHUNKS // PARTS * LANES
 
 
 def strain_table():
@@ -139,7 +140,8 @@
 
 
 def part_copy(src, dst, sems, part):
-    rows = pl.ds(part * PART_ROWS, min(PART_ROWS, CASES * ROWS - part * PART_ROWS))
+    start, stop = CUTS[part] * LANES, min(CUTS[part + 1] * LANES, CASES * ROWS)
+    rows = pl.ds(start, stop - start)
     return pltpu.make_async_copy(src.at[rows], dst.at[rows], sems.at[part])
 
 
@@ -149,16 +151,6 @@
     middle = rest.astype(jnp.bfloat16)
     low = (rest - middle.astype(jnp.float32)).astype(jnp.bfloat16)
     return high, middle, low
-
-
-def turn(choose, block):
-    high, middle, low = (
-        lax.dot_general(
-            choose, part, (((1,), (1,)), ((), ())), preferred_element_type=jnp.float32
-        )
-        for part in split_bf16(block)
-    )
-    return (high + middle) + low
 
 
 def pack_kernel(
@@ -193,17 +185,29 @@
     for copy in small:
         copy.wait()
     choose = ((state_slot_ref[...] >> 7) == owner).astype(jnp.float32).astype(jnp.bfloat16)
+    twice = jnp.concatenate([choose, choose], axis=1)
     home = (home_slot_ref[...] >> 7) == owner
     local = jnp.sum(jnp.where(home, lane, 0).astype(jnp.float32), axis=1, keepdims=True)
     extra = node_row(disp_ref, scratch, TAIL) + jnp.where(lane == TAIL + NODES, local, 0.0)
     held_ref[CASES * ROWS :, :] = jnp.zeros((WIDE - CASES * ROWS, LANES), jnp.float32)
     for part in range(PARTS):
         part_copy(state_ref, held_ref, sems, part).wait()
-        for k in range(part * CHUNKS // PARTS, (part + 1) * CHUNKS // PARTS):
-            turned = turn(choose, held_ref[k * LANES : (k + 1) * LANES, :])
-            if k == CHUNKS - 1:
-                turned = turned + extra
-            out_ref[pl.ds(k, DEV, stride=CHUNKS), :] = turned
+        for first in range(CUTS[part], CUTS[part + 1], STEP):
+            high, middle, low = split_bf16(held_ref[first * LANES : (first + STEP) * LANES, :])
+            picked = lax.dot_general(
+                jnp.concatenate([high, middle], axis=1),
+                twice,
+                (((1,), (1,)), ((), ())),
+                preferred_element_type=jnp.float32,
+            )
+            picked = picked + lax.dot_general(
+                low, choose, (((1,), (1,)), ((), ())), preferred_element_type=jnp.float32
+            )
+            for k in range(first, first + STEP):
+                turned = picked[(k - first) * LANES : (k - first + 1) * LANES].T
+                if k == CHUNKS - 1:
+                    turned = turned + extra
+                out_ref[pl.ds(k, DEV, stride=CHUNKS), :] = turned
 
 
 def macro_strain_rows(tail):
@@ -368,7 +372,7 @@
                 line = below
             return tuple(sums), work
 
-        return lax.fori_loop(0, R, plane, ((zero,) * 6, zero))
+        return lax.fori_loop(0, R, plane, ((zero,) * 6, zero), unroll=2)
 
     def force_pass(src, finish, dst):
         def plane(a, carry):
@@ -387,38 +391,36 @@
                             tile_at(sig_ref, behind, PAIRS[0][i] * VOX + at)
                             + tile_at(sig_ref, base, PAIRS[1][i] * VOX + pb * R + c)
                         ) + last[i]
-                        value = finish(come - gone, tile_at(src, base, i * VOX + at))
+                        value = finish(come, gone, tile_at(src, base, i * VOX + at))
                         dst[pl.ds(base + (i * VOX + at) * 8, 8), :] = value
                         totals[i] = totals[i] + value * value
                     last = [own[PAIRS[2][i]] for i in range(3)]
             return tuple(totals)
 
-        totals = lax.fori_loop(0, R, plane, (zero,) * 3)
+        totals = lax.fori_loop(0, R, plane, (zero,) * 3, unroll=2)
         return (totals[0] + totals[1]) + totals[2]
 
     mean0, _ = stress_pass(w_ref, imposed, True, False)
-    square0 = force_pass(w_ref, lambda div, w: -(div + STAB * w), p_ref)
+    square0 = force_pass(w_ref, lambda come, gone, w: (gone - come) - STAB * w, p_ref)
     saves[1].start()
     mean1, work1 = stress_pass(p_ref, None, True, True)
     step0 = square0 / (work1 + STAB * square0)
-    square1 = force_pass(p_ref, lambda div, p: p - step0 * (div + STAB * p), q_ref)
+    kept = 1.0 - STAB * step0
+    square1 = force_pass(p_ref, lambda come, gone, p: kept * p - step0 * (come - gone), q_ref)
     ratio = square1 / square0
 
     def direction(a, carry):
-        totals = list(carry)
         base = pl.multiple_of(a * 288, 8)
         for at in range(36):
             for i in range(3):
-                value = tile_at(q_ref, base, i * VOX + at) + ratio * tile_at(
-                    p_ref, base, i * VOX + at
-                )
-                q_ref[pl.ds(base + (i * VOX + at) * 8, 8), :] = value
-                totals[i] = totals[i] + value * value
+                q_ref[pl.ds(base + (i * VOX + at) * 8, 8), :] = tile_at(
+                    q_ref, base, i * VOX + at
+                ) + ratio * tile_at(p_ref, base, i * VOX + at)
         save_plane(base)
-        return tuple(totals)
-
-    totals = lax.fori_loop(0, R, direction, (zero,) * 3)
-    length = (totals[0] + totals[1]) + totals[2]
+        return carry
+
+    lax.fori_loop(0, R, direction, 0)
+    length = square1 + ratio * square1
     mean2, work2 = stress_pass(q_ref, None, False, True)
     step1 = square1 / (work2 + STAB * length)
     step_ref[0:8, :] = step0
@@ -554,21 +556,18 @@
     return lax.all_to_all(value, AXES, split_axis=0, concat_axis=0, tiled=True)
 
 
-def per_device(displacement, load, home_slot, micro_state, state_slot, phases, phase_moduli):
-    force_table, weight_table, place_table = assembly_tables()
-    f32 = jnp.float32
-    home_row = home_slot.reshape(1, LANES)
-    sent = pl.pallas_call(
+def run_pack(micro_state, state_slot, home_slot, displacement):
+    return pl.pallas_call(
         pack_kernel,
-        out_shape=jax.ShapeDtypeStruct((DEV * CHUNKS, LANES), f32),
+        out_shape=jax.ShapeDtypeStruct((DEV * CHUNKS, LANES), jnp.float32),
         in_specs=[HBM] * 4,
         out_specs=VMEM,
         scratch_shapes=[
-            pltpu.VMEM((WIDE, LANES), f32),
+            pltpu.VMEM((WIDE, LANES), jnp.float32),
             pltpu.VMEM((1, LANES), jnp.int32),
             pltpu.VMEM((1, LANES), jnp.int32),
-            pltpu.VMEM(displacement.shape, f32),
-            pltpu.VMEM((8, LANES), f32),
+            pltpu.VMEM(displacement.shape, jnp.float32),
+            pltpu.VMEM((8, LANES), jnp.float32),
             pltpu.SemaphoreType.DMA((PARTS + 3,)),
         ],
         compiler_params=pltpu.CompilerParams(vmem_limit_bytes=12 << 20),
@@ -576,12 +575,15 @@
     )(
         in_hbm(micro_state.reshape(CASES * ROWS, LANES)),
         in_hbm(state_slot.reshape(1, LANES)),
-        in_hbm(home_row),
+        in_hbm(home_slot.reshape(1, LANES)),
         in_hbm(displacement),
     )
-    received = exchange(sent.reshape(DEV, 1, WIDE)).reshape(DEV * CHUNKS, LANES)
+
+
+def run_solve(received, phases, phase_moduli, home_slot, load):
+    f32 = jnp.float32
     big = pltpu.HBM((ROWS * 8, LANES), f32)
-    answer, w, p, q, steps = pl.pallas_call(
+    return pl.pallas_call(
         solve_kernel,
         out_shape=(
             jax.ShapeDtypeStruct((DEV * 8, LANES), f32),
@@ -605,11 +607,13 @@
         ],
         compiler_params=pltpu.CompilerParams(vmem_limit_bytes=32 << 20),
         name="solve",
-    )(received, phases, phase_moduli, home_row, load)
-    returned = exchange(answer.reshape(DEV, 8, LANES)).reshape(DEV * 8, LANES)
-    new_state = pl.pallas_call(
+    )(received, phases, phase_moduli, home_slot.reshape(1, LANES), load)
+
+
+def run_update(w, p, q, steps):
+    return pl.pallas_call(
         update_kernel,
-        out_shape=jax.ShapeDtypeStruct((CASES, ROWS, LANES), f32),
+        out_shape=jax.ShapeDtypeStruct((CASES, ROWS, LANES), jnp.float32),
         grid=(ROWS // UPDATE,),
         in_specs=[pl.BlockSpec((UPDATE * 8, LANES), lambda k: (k, 0))] * 3
         + [pl.BlockSpec((16, LANES), lambda k: (0, 0))],
@@ -620,14 +624,17 @@
         ),
         name="update",
     )(in_hbm(w), in_hbm(p), in_hbm(q), steps)
-    me = lax.axis_index(AXES).astype(jnp.int32).reshape(1, 1)
-    node_shape = jax.ShapeDtypeStruct(displacement.shape, f32)
-    displaced, residual, rel_norm = pl.pallas_call(
+
+
+def run_final(returned, me, displacement):
+    force_table, weight_table, place_table = assembly_tables()
+    node_shape = jax.ShapeDtypeStruct(displacement.shape, jnp.float32)
+    return pl.pallas_call(
         final_kernel,
-        out_shape=(node_shape, node_shape, jax.ShapeDtypeStruct((1, 1), f32)),
+        out_shape=(node_shape, node_shape, jax.ShapeDtypeStruct((1, 1), jnp.float32)),
         in_specs=[VMEM, SMEM, VMEM, VMEM, VMEM, VMEM],
         out_specs=[VMEM] * 3,
-        scratch_shapes=[pltpu.VMEM((8, LANES), f32)],
+        scratch_shapes=[pltpu.VMEM((8, LANES), jnp.float32)],
         compiler_params=pltpu.CompilerParams(vmem_limit_bytes=12 << 20),
         name="final",
     )(
@@ -638,6 +645,16 @@
         jnp.asarray(weight_table),
         jnp.asarray(place_table),
     )
+
+
+def per_device(displacement, load, home_slot, micro_state, state_slot, phases, phase_moduli):
+    sent = run_pack(micro_state, state_slot, home_slot, displacement)
+    received = exchange(sent.reshape(DEV, 1, WIDE)).reshape(DEV * CHUNKS, LANES)
+    answer, w, p, q, steps = run_solve(received, phases, phase_moduli, home_slot, load)
+    returned = exchange(answer.reshape(DEV, 8, LANES)).reshape(DEV * 8, LANES)
+    new_state = run_update(w, p, q, steps)
+    me = lax.axis_index(AXES).astype(jnp.int32).reshape(1, 1)
+    displaced, residual, rel_norm = run_final(returned, me, displacement)
     return (
         new_state.reshape(micro_state.shape),
         displaced,

time: 78.7 us -> 77.4 us (0.983)
  Pallas kernels: 23.4 us -> 22 us
    pallas_call x4, Pallas kernels: 23.4 us -> 22 us  [the longest x1 8.69 us: run_solve(): pl.pallas_call(solve_kernel, out_shape=(jax.ShapeDtypeStruct((DEV * 8, LA...]
  transfers between devices with their start and end apart: 1 -> 1, of which waited for: 1 -> 1; matrix products, arithmetic and copies ran while one was open for 0% -> 0% of each run, Pallas kernels for 10% -> 11%
where the time goes in v3:
time: 77.4 us; the launch traced here: 77 us
  blocking collectives  42.6 us (55%)
  Pallas kernels  22 us (28%)
  starting transfers between devices  6.32 us (8%)
  waiting for transfers between devices  5.25 us (7%)
    all_to_all x1, blocking collectives, exchange(): return lax.all_to_all(value, AXES, split_axis=0, concat_axis=0, tiled=True)  42.6 us
    pallas_call x1, Pallas kernels, run_solve(): pl.pallas_call(solve_kernel, out_shape=(jax.ShapeDtypeStruct((DEV * 8, LA...  8.69 us
    pallas_call x1, Pallas kernels, run_update(): pl.pallas_call(update_kernel, out_shape=jax.ShapeDtypeStruct((CASES, ROWS...  8.18 us
    all_to_all x1, starting transfers between devices, exchange(): return lax.all_to_all(value, AXES, split_axis=0, concat_axis=0, tiled=True)  6.32 us
    all_to_all x1, waiting for transfers between devices, exchange(): return lax.all_to_all(value, AXES, split_axis=0, concat_axis=0, tiled=True)  5.25 us
    pallas_call x1, Pallas kernels, run_pack(): pl.pallas_call(pack_kernel, out_shape=jax.ShapeDtypeStruct((DEV * CHUNKS,...  3.36 us
    pallas_call x1, Pallas kernels, run_final(): pl.pallas_call(final_kernel, out_shape=(node_shape, node_shape, jax.Shape...  1.79 us
  transfers between devices with their start and end apart: 1, of which 1 were waited for; matrix products, arithmetic and copies ran while one was open for 0% of the time, Pallas kernels for 11%

profile of v3, /device:TPU:1, one launch (start us, length us, event | category | flops | bytes accessed | tf_op | source)
XLA Modules:
  0.0 77.0 jit_solution(10829606144425589001)
XLA Ops:
  0.6 3.4 %pack.1 = f32[4608,128]{1,0:T(8,128)S(1)} custom-call(f32[4536,128]{1,0:T(8,128)} %bitcast.16, s32[1,128]{1,0:T(1,128)} %bitcast.17, s32[1,128]{1,0:T(1,128)} %bitcast.13, f32[3,1,2,8]{3,2,1,0:T(2,128)} %disp_ref.1), custom_call_target="tpu_custom_call" | custom-call | tf_op jit(solution)/shard_map/pack/pallas_call | solution.py:560
  4.0 0.0 copy-start.2
  4.0 0.0 copy-start.5
  4.0 0.0 copy-start.6
  4.0 0.0 copy-start.7
  4.0 42.6 %all_to_all.10 = f32[128,1,4608]{2,1,0:T(1,128)S(1)} all-to-all(f32[128,1,4608]{2,1,0:T(1,128)S(1)} %bitcast.11), channel_id=1, replica_groups=mesh['far'=16,'core'=2,'rve'=4] {'core','far','rve'}, dimensions={0} | all-to-all | bytes 4718592 | tf_op jit(solution)/shard_map/all_to_all | solution.py:556
  46.6 0.0 copy-done.2
  46.6 0.0 copy-done.5
  46.7 0.0 copy-done.6
  46.7 0.0 copy-done.7
  46.7 8.7 %solve.1 = (f32[1024,128]{1,0:T(8,128)}, f32[5184,128]{1,0:T(8,128)}, f32[5184,128]{1,0:T(8,128)}, f32[5184,128]{1,0:T(8,128)}, f32[16,128]{1,0:T(8,128)S(1)}) custom-call(f32[4608,128]{1,0:T(8,128)S(1)} %bitcast.10, s32[216,128]{1,0:T(8,128)S(1)} %copy-done.2, f32[2,3]{1,0:T(2,128)S(1)} %copy-done.7, s32[1,128]{1,0:T(1,128)S(1)} %bitcast.14, ...), custom_call_target="tpu_custom_call" | custom-call | tf_op jit(solution)/shard_map/solve/pallas_call | solution.py:586
  55.4 6.3 %all-to-all-start.1 = ((f32[128,8,128]{2,1,0:T(8,128)}), f32[128,8,128]{2,1,0:T(8,128)S(1)}, u32[]{:S(2)}, u32[]{:S(2)}) async-start(f32[128,8,128]{2,1,0:T(8,128)} %bitcast.6), calls=%async_computation.1 | async-start | bytes 1048576 | tf_op jit(solution)/shard_map/all_to_all | solution.py:556
  61.7 0.0 copy-start
  61.7 0.0 copy-start.1
  61.7 0.0 copy-start.3
  61.7 0.0 copy-start.4
  61.8 8.2 %update.1 = f32[7,648,128]{2,1,0:T(8,128)} custom-call(f32[5184,128]{1,0:T(8,128)} %get-tuple-element.12.w_ref, f32[5184,128]{1,0:T(8,128)} %get-tuple-element.13.p_ref, f32[5184,128]{1,0:T(8,128)} %get-tuple-element.14.q_ref, f32[16,128]{1,0:T(8,128)S(1)} %get-tuple-element.15.step_ref), custom_call_target="tpu_custom_call" | custom-call | flops 20000000 | bytes 10000000 | tf_op jit(solution)/shard_map/update/pallas_call | solution.py:614
  69.9 5.3 %all-to-all-done.1 = f32[128,8,128]{2,1,0:T(8,128)S(1)} async-done(((f32[128,8,128]{2,1,0:T(8,128)}), f32[128,8,128]{2,1,0:T(8,128)S(1)}, u32[]{:S(2)}, u32[]{:S(2)}) %all-to-all-start.1) | async-done | bytes 524320 | tf_op jit(solution)/shard_map/all_to_all | solution.py:556
  75.2 0.0 copy-done
  75.2 0.0 copy-done.1
  75.2 0.0 copy-done.3
  75.2 0.0 copy-done.4
  75.2 1.8 %final.1 = (f32[3,1,2,8]{3,2,1,0:T(2,128)}, f32[3,1,2,8]{3,2,1,0:T(2,128)}, f32[1,1]{1,0:T(1,128)}) custom-call(f32[1024,128]{1,0:T(8,128)S(1)} %bitcast.12, s32[1,1]{1,0:T(1,128)} %bitcast.8.me_ref, f32[3,1,2,8]{3,2,1,0:T(2,128)S(1)} %copy-done.4, f32[768,256]{1,0:T(8,128)S(1)} %copy-done, f32[144,128]{1,0:T(8,128)S(1)} %copy-done.3, ...), custom_call_target="tpu_custom_call" | custom-call | tf_op jit(solution)/shard_map/final/pallas_call | solution.py:632
Async XLA Ops:
  4.0 42.6 %copy-start.2 = (s32[216,128]{1,0:T(8,128)S(1)}, s32[216,128]{1,0:T(8,128)}, u32[]{:S(2)}) copy-start(s32[216,128]{1,0:T(8,128)} %phase_ref.1) | copy-start | bytes 331780
  4.0 42.6 %copy-start.5 = (f32[3,1,2,8]{3,2,1,0:T(2,128)S(1)}, f32[3,1,2,8]{3,2,1,0:T(2,128)}, u32[]{:S(2)}) copy-start(f32[3,1,2,8]{3,2,1,0:T(2,128)} %load_ref.1) | copy-start | bytes 580
  4.0 42.6 %copy-start.6 = (s32[128]{0:T(128)S(1)}, s32[128]{0:T(128)}, u32[]{:S(2)}) copy-start(s32[128]{0:T(128)} %param.12) | copy-start | bytes 1540
  4.0 42.6 %copy-start.7 = (f32[2,3]{1,0:T(2,128)S(1)}, f32[2,3]{1,0:T(2,128)}, u32[]{:S(2)}) copy-start(f32[2,3]{1,0:T(2,128)} %moduli_ref.1) | copy-start | bytes 76
  55.4 19.8 %all-to-all-start.1 = ((f32[128,8,128]{2,1,0:T(8,128)}), f32[128,8,128]{2,1,0:T(8,128)S(1)}, u32[]{:S(2)}, u32[]{:S(2)}) async-start(f32[128,8,128]{2,1,0:T(8,128)} %bitcast.6), calls=%async_computation.1 | async-start | bytes 1048576 | tf_op jit(solution)/shard_map/all_to_all | solution.py:556
  61.7 13.5 %copy-start = (f32[768,256]{1,0:T(8,128)S(1)}, f32[768,256]{1,0:T(8,128)}, u32[]{:S(2)}) copy-start(f32[768,256]{1,0:T(8,128)} %constant.24.clone.force_ref) | copy-start | bytes 2359300
  61.7 13.5 %copy-start.1 = (f32[4,128,128]{2,1,0:T(8,128)S(1)}, f32[4,128,128]{2,1,0:T(8,128)}, u32[]{:S(2)}) copy-start(f32[4,128,128]{2,1,0:T(8,128)} %constant.26.clone.place_ref) | copy-start | bytes 786436
  61.7 13.5 %copy-start.3 = (f32[144,128]{1,0:T(8,128)S(1)}, f32[144,128]{1,0:T(8,128)}, u32[]{:S(2)}) copy-start(f32[144,128]{1,0:T(8,128)} %constant.25.clone.weight_ref) | copy-start | bytes 221188
  61.7 13.5 %copy-start.4 = (f32[3,1,2,8]{3,2,1,0:T(2,128)S(1)}, f32[3,1,2,8]{3,2,1,0:T(2,128)}, u32[]{:S(2)}) copy-start(f32[3,1,2,8]{3,2,1,0:T(2,128)} %disp_ref.1) | copy-start | bytes 580

commit v4 on v3

--- a/solution.py
+++ b/solution.py
@@ -33,7 +33,7 @@
 VMEM = pl.BlockSpec(memory_space=pltpu.VMEM)
 SMEM = pl.BlockSpec(memory_space=pltpu.SMEM)
 HBM = pl.BlockSpec(memory_space=pltpu.HBM)
-CUTS = (0, 18, 30, 36)
+CUTS = (0, 6, 36)
 PARTS = len(CUTS) - 1
 STEP = 6
 UPDATE = 72
@@ -151,6 +151,16 @@
     middle = rest.astype(jnp.bfloat16)
     low = (rest - middle.astype(jnp.float32)).astype(jnp.bfloat16)
     return high, middle, low
+
+
+def flip(same, block):
+    high, middle, low = (
+        lax.dot_general(
+            same, part, (((1,), (1,)), ((), ())), preferred_element_type=jnp.float32
+        )
+        for part in split_bf16(block)
+    )
+    return (high + middle) + low
 
 
 def pack_kernel(
@@ -293,17 +303,19 @@
     zero = jnp.zeros((8, LANES), jnp.float32)
     phase = jnp.take_along_axis(phase_ref[...], device_at(lane_iota(VOX)), axis=1)
     mu = jnp.where(
-        phase == 0, moduli_ref[1, 0], jnp.where(phase == 1, moduli_ref[1, 1], moduli_ref[1, 2])
+        phase == 0, moduli_ref[1:2, 0:1], jnp.where(phase == 1, moduli_ref[1:2, 1:2], moduli_ref[1:2, 2:3])
     )
     lam_ref[...] = jnp.where(
-        phase == 0, moduli_ref[0, 0], jnp.where(phase == 1, moduli_ref[0, 1], moduli_ref[0, 2])
+        phase == 0, moduli_ref[0:1, 0:1], jnp.where(phase == 1, moduli_ref[0:1, 1:2], moduli_ref[0:1, 2:3])
     )
     mu_ref[...] = mu
     mu2_ref[...] = mu + mu
     w_ref[pl.ds(7, ROWS, stride=8), :] = jnp.zeros((ROWS, LANES), jnp.float32)
     tail = None
+    same = (sublane_iota(DEV) == lane_iota(DEV)).astype(jnp.float32).astype(jnp.bfloat16)
     for k in range(CHUNKS):
-        turned = recv_ref[pl.ds(k, DEV, stride=CHUNKS), :].T
+        block = recv_ref[pl.ds(k, DEV, stride=CHUNKS), :]
+        turned = flip(same, block) if k % 3 == 1 else block.T
         start, stop = k * LANES, min((k + 1) * LANES, CASES * ROWS)
         while start < stop:
             case = start // ROWS
@@ -483,7 +495,7 @@
     norm_ref,
     scratch,
 ):
-    me = me_ref[0, 0]
+    me = me_ref[...]
     order = recv_ref[pl.ds(6, DEV, stride=8), :].astype(jnp.int32)
     special = recv_ref[pl.ds(7, DEV, stride=8), :]
     stress = [
@@ -592,7 +604,7 @@
             big,
             jax.ShapeDtypeStruct((16, LANES), f32),
         ),
-        in_specs=[VMEM, VMEM, SMEM, VMEM, VMEM],
+        in_specs=[VMEM, VMEM, VMEM, VMEM, VMEM],
         out_specs=[VMEM, HBM, HBM, HBM, VMEM],
         scratch_shapes=[
             pltpu.VMEM((ROWS * 8, LANES), f32),
@@ -632,7 +644,7 @@
     return pl.pallas_call(
         final_kernel,
         out_shape=(node_shape, node_shape, jax.ShapeDtypeStruct((1, 1), jnp.float32)),
-        in_specs=[VMEM, SMEM, VMEM, VMEM, VMEM, VMEM],
+        in_specs=[VMEM] * 6,
         out_specs=[VMEM] * 3,
         scratch_shapes=[pltpu.VMEM((8, LANES), jnp.float32)],
         compiler_params=pltpu.CompilerParams(vmem_limit_bytes=12 << 20),
@@ -653,7 +665,7 @@
     answer, w, p, q, steps = run_solve(received, phases, phase_moduli, home_slot, load)
     returned = exchange(answer.reshape(DEV, 8, LANES)).reshape(DEV * 8, LANES)
     new_state = run_update(w, p, q, steps)
-    me = lax.axis_index(AXES).astype(jnp.int32).reshape(1, 1)
+    me = jnp.full((1, LANES), lax.axis_index(AXES), jnp.int32)
     displaced, residual, rel_norm = run_final(returned, me, displacement)
     return (
         new_state.reshape(micro_state.shape),

time: 77.4 us -> 76.3 us (0.986)
  Pallas kernels: 22 us -> 20.9 us
where the time goes in v4:
time: 76.3 us; the launch traced here: 75.9 us
  blocking collectives  42.6 us (56%)
  Pallas kernels  20.9 us (27%)
  starting transfers between devices  6.32 us (8%)
  waiting for transfers between devices  5.25 us (7%)
    all_to_all x1, blocking collectives, exchange(): return lax.all_to_all(value, AXES, split_axis=0, concat_axis=0, tiled=True)  42.6 us
    pallas_call x1, Pallas kernels, run_update(): pl.pallas_call(update_kernel, out_shape=jax.ShapeDtypeStruct((CASES, ROWS...  8.18 us
    pallas_call x1, Pallas kernels, run_solve(): pl.pallas_call(solve_kernel, out_shape=(jax.ShapeDtypeStruct((DEV * 8, LA...  8.01 us
    all_to_all x1, starting transfers between devices, exchange(): return lax.all_to_all(value, AXES, split_axis=0, concat_axis=0, tiled=True)  6.32 us
    all_to_all x1, waiting for transfers between devices, exchange(): return lax.all_to_all(value, AXES, split_axis=0, concat_axis=0, tiled=True)  5.25 us
    pallas_call x1, Pallas kernels, run_pack(): pl.pallas_call(pack_kernel, out_shape=jax.ShapeDtypeStruct((DEV * CHUNKS,...  2.94 us
    pallas_call x1, Pallas kernels, run_final(): pl.pallas_call(final_kernel, out_shape=(node_shape, node_shape, jax.Shape...  1.79 us
  transfers between devices with their start and end apart: 1, of which 1 were waited for; matrix products, arithmetic and copies ran while one was open for 0% of the time, Pallas kernels for 11%

profile of v4, /device:TPU:1, one launch (start us, length us, event | category | flops | bytes accessed | tf_op | source)
XLA Modules:
  0.0 75.9 jit_solution(12848830193501526980)
XLA Ops:
  0.6 2.9 %pack.1 = f32[4608,128]{1,0:T(8,128)S(1)} custom-call(f32[4536,128]{1,0:T(8,128)} %bitcast.15, s32[1,128]{1,0:T(1,128)} %bitcast.16, s32[1,128]{1,0:T(1,128)} %bitcast.12, f32[3,1,2,8]{3,2,1,0:T(2,128)} %disp_ref.1), custom_call_target="tpu_custom_call" | custom-call | tf_op jit(solution)/shard_map/pack/pallas_call | solution.py:572
  3.6 0.0 copy-start.2
  3.6 0.0 copy-start.5
  3.6 0.0 copy-start.6
  3.6 0.0 copy-start.7
  3.6 42.6 %all_to_all.10 = f32[128,1,4608]{2,1,0:T(1,128)S(1)} all-to-all(f32[128,1,4608]{2,1,0:T(1,128)S(1)} %bitcast.10), channel_id=1, replica_groups=mesh['far'=16,'core'=2,'rve'=4] {'core','far','rve'}, dimensions={0} | all-to-all | bytes 4718592 | tf_op jit(solution)/shard_map/all_to_all | solution.py:568
  46.2 0.0 copy-done.2
  46.2 0.0 copy-done.5
  46.2 0.0 copy-done.6
  46.2 0.0 copy-done.7
  46.2 8.0 %solve.1 = (f32[1024,128]{1,0:T(8,128)}, f32[5184,128]{1,0:T(8,128)}, f32[5184,128]{1,0:T(8,128)}, f32[5184,128]{1,0:T(8,128)}, f32[16,128]{1,0:T(8,128)S(1)}) custom-call(f32[4608,128]{1,0:T(8,128)S(1)} %bitcast.9, s32[216,128]{1,0:T(8,128)S(1)} %copy-done.2, f32[2,3]{1,0:T(2,128)S(1)} %copy-done.7, s32[1,128]{1,0:T(1,128)S(1)} %bitcast.13, ...), custom_call_target="tpu_custom_call" | custom-call | tf_op jit(solution)/shard_map/solve/pallas_call | solution.py:598
  54.3 6.3 %all-to-all-start.1 = ((f32[128,8,128]{2,1,0:T(8,128)}), f32[128,8,128]{2,1,0:T(8,128)S(1)}, u32[]{:S(2)}, u32[]{:S(2)}) async-start(f32[128,8,128]{2,1,0:T(8,128)} %bitcast.6), calls=%async_computation.1 | async-start | bytes 1048576 | tf_op jit(solution)/shard_map/all_to_all | solution.py:568
  60.6 0.0 copy-start
  60.6 0.0 copy-start.1
  60.6 0.0 copy-start.3
  60.6 0.0 copy-start.4
  60.7 8.2 %update.1 = f32[7,648,128]{2,1,0:T(8,128)} custom-call(f32[5184,128]{1,0:T(8,128)} %get-tuple-element.12.w_ref, f32[5184,128]{1,0:T(8,128)} %get-tuple-element.13.p_ref, f32[5184,128]{1,0:T(8,128)} %get-tuple-element.14.q_ref, f32[16,128]{1,0:T(8,128)S(1)} %get-tuple-element.15.step_ref), custom_call_target="tpu_custom_call" | custom-call | flops 20000000 | bytes 10000000 | tf_op jit(solution)/shard_map/update/pallas_call | solution.py:626
  68.8 5.3 %all-to-all-done.1 = f32[128,8,128]{2,1,0:T(8,128)S(1)} async-done(((f32[128,8,128]{2,1,0:T(8,128)}), f32[128,8,128]{2,1,0:T(8,128)S(1)}, u32[]{:S(2)}, u32[]{:S(2)}) %all-to-all-start.1) | async-done | bytes 524320 | tf_op jit(solution)/shard_map/all_to_all | solution.py:568
  74.1 0.0 copy-done
  74.1 0.0 copy-done.1
  74.1 0.0 copy-done.3
  74.1 0.0 copy-done.4
  74.1 1.8 %final.1 = (f32[3,1,2,8]{3,2,1,0:T(2,128)}, f32[3,1,2,8]{3,2,1,0:T(2,128)}, f32[1,1]{1,0:T(1,128)}) custom-call(f32[1024,128]{1,0:T(8,128)S(1)} %bitcast.11, s32[1,128]{1,0:T(1,128)S(1)} %broadcast_in_dim.3.me_ref, f32[3,1,2,8]{3,2,1,0:T(2,128)S(1)} %copy-done.4, f32[768,256]{1,0:T(8,128)S(1)} %copy-done, f32[144,128]{1,0:T(8,128)S(1)} %copy-done.3, ...), custom_call_target="tpu_custom_call" | custom-call | tf_op jit(solution)/shard_map/final/pallas_call | solution.py:644
  (1 shorter events, 0.0 us)
Async XLA Ops:
  3.6 42.6 %copy-start.2 = (s32[216,128]{1,0:T(8,128)S(1)}, s32[216,128]{1,0:T(8,128)}, u32[]{:S(2)}) copy-start(s32[216,128]{1,0:T(8,128)} %phase_ref.1) | copy-start | bytes 331780
  3.6 42.6 %copy-start.5 = (f32[3,1,2,8]{3,2,1,0:T(2,128)S(1)}, f32[3,1,2,8]{3,2,1,0:T(2,128)}, u32[]{:S(2)}) copy-start(f32[3,1,2,8]{3,2,1,0:T(2,128)} %load_ref.1) | copy-start | bytes 580
  3.6 42.6 %copy-start.6 = (s32[128]{0:T(128)S(1)}, s32[128]{0:T(128)}, u32[]{:S(2)}) copy-start(s32[128]{0:T(128)} %param.12) | copy-start | bytes 1540
  3.6 42.6 %copy-start.7 = (f32[2,3]{1,0:T(2,128)S(1)}, f32[2,3]{1,0:T(2,128)}, u32[]{:S(2)}) copy-start(f32[2,3]{1,0:T(2,128)} %moduli_ref.1) | copy-start | bytes 76
  54.3 19.8 %all-to-all-start.1 = ((f32[128,8,128]{2,1,0:T(8,128)}), f32[128,8,128]{2,1,0:T(8,128)S(1)}, u32[]{:S(2)}, u32[]{:S(2)}) async-start(f32[128,8,128]{2,1,0:T(8,128)} %bitcast.6), calls=%async_computation.1 | async-start | bytes 1048576 | tf_op jit(solution)/shard_map/all_to_all | solution.py:568
  60.6 13.5 %copy-start = (f32[768,256]{1,0:T(8,128)S(1)}, f32[768,256]{1,0:T(8,128)}, u32[]{:S(2)}) copy-start(f32[768,256]{1,0:T(8,128)} %constant.24.clone.force_ref) | copy-start | bytes 2359300
  60.6 13.5 %copy-start.1 = (f32[4,128,128]{2,1,0:T(8,128)S(1)}, f32[4,128,128]{2,1,0:T(8,128)}, u32[]{:S(2)}) copy-start(f32[4,128,128]{2,1,0:T(8,128)} %constant.26.clone.place_ref) | copy-start | bytes 786436
  60.6 13.5 %copy-start.3 = (f32[144,128]{1,0:T(8,128)S(1)}, f32[144,128]{1,0:T(8,128)}, u32[]{:S(2)}) copy-start(f32[144,128]{1,0:T(8,128)} %constant.25.clone.weight_ref) | copy-start | bytes 221188
  60.6 13.5 %copy-start.4 = (f32[3,1,2,8]{3,2,1,0:T(2,128)S(1)}, f32[3,1,2,8]{3,2,1,0:T(2,128)}, u32[]{:S(2)}) copy-start(f32[3,1,2,8]{3,2,1,0:T(2,128)} %disp_ref.1) | copy-start | bytes 580

commit v5 on v4

--- a/solution.py
+++ b/solution.py
@@ -36,7 +36,7 @@
 CUTS = (0, 6, 36)
 PARTS = len(CUTS) - 1
 STEP = 6
-UPDATE = 72
+PITCH = ROWS + 1
 
 
 def strain_table():
@@ -276,10 +276,7 @@
     slot_ref,
     load_ref,
     ret_ref,
-    w_out,
-    p_out,
-    q_out,
-    step_ref,
+    new_ref,
     w_ref,
     p_ref,
     q_ref,
@@ -288,18 +285,7 @@
     mu_ref,
     mu2_ref,
     scratch,
-    sems,
 ):
-    saves = [
-        pltpu.make_async_copy(src, dst, sems.at[k])
-        for k, (src, dst) in enumerate(((w_ref, w_out), (p_ref, p_out), (q_ref, q_out)))
-    ]
-
-    def save_plane(base):
-        for i in range(3):
-            rows = pl.ds(base + i * VOX * 8, 288)
-            pltpu.make_async_copy(q_ref.at[rows], q_out.at[rows], sems.at[2]).start()
-
     zero = jnp.zeros((8, LANES), jnp.float32)
     phase = jnp.take_along_axis(phase_ref[...], device_at(lane_iota(VOX)), axis=1)
     mu = jnp.where(
@@ -325,7 +311,6 @@
             ]
             start = end
         tail = turned
-    saves[0].start()
     macro = macro_strain_rows(tail)
     sub = sublane_iota()
     imposed = [
@@ -414,7 +399,6 @@
 
     mean0, _ = stress_pass(w_ref, imposed, True, False)
     square0 = force_pass(w_ref, lambda come, gone, w: (gone - come) - STAB * w, p_ref)
-    saves[1].start()
     mean1, work1 = stress_pass(p_ref, None, True, True)
     step0 = square0 / (work1 + STAB * square0)
     kept = 1.0 - STAB * step0
@@ -428,15 +412,29 @@
                 q_ref[pl.ds(base + (i * VOX + at) * 8, 8), :] = tile_at(
                     q_ref, base, i * VOX + at
                 ) + ratio * tile_at(p_ref, base, i * VOX + at)
-        save_plane(base)
         return carry
 
     lax.fori_loop(0, R, direction, 0)
     length = square1 + ratio * square1
     mean2, work2 = stress_pass(q_ref, None, False, True)
     step1 = square1 / (work2 + STAB * length)
-    step_ref[0:8, :] = step0
-    step_ref[8:16, :] = step1
+    place = place_of(lane_iota(8))
+
+    def update(a, carry):
+        base = pl.multiple_of(a * 288, 8)
+        for i in range(3):
+            for at in range(36):
+                value = (
+                    tile_at(w_ref, base, i * VOX + at)
+                    + step0 * tile_at(p_ref, base, i * VOX + at)
+                    + step1 * tile_at(q_ref, base, i * VOX + at)
+                )
+                new_ref[pl.ds(a * 36 + i * VOX + at, 8, stride=PITCH), :] = jnp.take_along_axis(
+                    value, place, axis=1
+                )
+        return carry
+
+    lax.fori_loop(0, R, update, 0)
     mean = [(mean0[m] + step0 * mean1[m] + step1 * mean2[m]) * (1.0 / VOX) for m in range(6)]
 
     shared = place_of(slot_ref[...] >> 7).astype(jnp.float32)
@@ -456,18 +454,6 @@
     for peer in range(DEV):
         ret_ref[8 * peer : 8 * peer + 8, :] = shared
     ret_ref[pl.ds(7, DEV, stride=8), :] = special
-    for save in saves:
-        save.wait()
-
-
-def update_kernel(w_ref, p_ref, q_ref, step_ref, out_ref):
-    place = place_of(lane_iota(UPDATE))
-    for case in range(CASES):
-        first = step_ref[case : case + 1, :]
-        second = step_ref[8 + case : 9 + case, :]
-        rows = pl.ds(case, UPDATE, stride=8)
-        value = w_ref[rows, :] + first * p_ref[rows, :] + second * q_ref[rows, :]
-        out_ref[case] = jnp.take_along_axis(value, place, axis=1)
 
 
 def row_of(value, index):
@@ -490,11 +476,22 @@
     force_ref,
     weight_ref,
     place_ref,
+    state_ref,
     new_disp_ref,
     res_ref,
     norm_ref,
+    state_out,
     scratch,
+    sems,
 ):
+    saves = [
+        pltpu.make_async_copy(
+            state_ref.at[pl.ds(case * PITCH, ROWS)], state_out.at[case], sems.at[case]
+        )
+        for case in range(CASES)
+    ]
+    for save in saves:
+        save.start()
     me = me_ref[...]
     order = recv_ref[pl.ds(6, DEV, stride=8), :].astype(jnp.int32)
     special = recv_ref[pl.ds(7, DEV, stride=8), :]
@@ -558,6 +555,8 @@
         tile = node_tile(value)
         for i in range(3):
             ref[i, 0] = tile[2 * i : 2 * i + 2, 0:8]
+    for save in saves:
+        save.wait()
 
 
 def in_hbm(value):
@@ -594,18 +593,14 @@
 
 def run_solve(received, phases, phase_moduli, home_slot, load):
     f32 = jnp.float32
-    big = pltpu.HBM((ROWS * 8, LANES), f32)
     return pl.pallas_call(
         solve_kernel,
         out_shape=(
             jax.ShapeDtypeStruct((DEV * 8, LANES), f32),
-            big,
-            big,
-            big,
-            jax.ShapeDtypeStruct((16, LANES), f32),
+            jax.ShapeDtypeStruct((8 * PITCH, LANES), f32),
         ),
         in_specs=[VMEM, VMEM, VMEM, VMEM, VMEM],
-        out_specs=[VMEM, HBM, HBM, HBM, VMEM],
+        out_specs=[VMEM] * 2,
         scratch_shapes=[
             pltpu.VMEM((ROWS * 8, LANES), f32),
             pltpu.VMEM((ROWS * 8, LANES), f32),
@@ -615,38 +610,29 @@
             pltpu.VMEM((VOX, LANES), f32),
             pltpu.VMEM((VOX, LANES), f32),
             pltpu.VMEM((8, LANES), f32),
-            pltpu.SemaphoreType.DMA((3,)),
         ],
         compiler_params=pltpu.CompilerParams(vmem_limit_bytes=32 << 20),
         name="solve",
     )(received, phases, phase_moduli, home_slot.reshape(1, LANES), load)
 
 
-def run_update(w, p, q, steps):
-    return pl.pallas_call(
-        update_kernel,
-        out_shape=jax.ShapeDtypeStruct((CASES, ROWS, LANES), jnp.float32),
-        grid=(ROWS // UPDATE,),
-        in_specs=[pl.BlockSpec((UPDATE * 8, LANES), lambda k: (k, 0))] * 3
-        + [pl.BlockSpec((16, LANES), lambda k: (0, 0))],
-        out_specs=pl.BlockSpec((CASES, UPDATE, LANES), lambda k: (0, k, 0)),
-        compiler_params=pltpu.CompilerParams(vmem_limit_bytes=8 << 20),
-        cost_estimate=pl.CostEstimate(
-            flops=20_000_000, bytes_accessed=10_000_000, transcendentals=0
-        ),
-        name="update",
-    )(in_hbm(w), in_hbm(p), in_hbm(q), steps)
-
-
-def run_final(returned, me, displacement):
+def run_final(returned, me, displacement, state):
     force_table, weight_table, place_table = assembly_tables()
     node_shape = jax.ShapeDtypeStruct(displacement.shape, jnp.float32)
     return pl.pallas_call(
         final_kernel,
-        out_shape=(node_shape, node_shape, jax.ShapeDtypeStruct((1, 1), jnp.float32)),
-        in_specs=[VMEM] * 6,
-        out_specs=[VMEM] * 3,
-        scratch_shapes=[pltpu.VMEM((8, LANES), jnp.float32)],
+        out_shape=(
+            node_shape,
+            node_shape,
+            jax.ShapeDtypeStruct((1, 1), jnp.float32),
+            pltpu.HBM((CASES, ROWS, LANES), jnp.float32),
+        ),
+        in_specs=[VMEM] * 7,
+        out_specs=[VMEM] * 3 + [HBM],
+        scratch_shapes=[
+            pltpu.VMEM((8, LANES), jnp.float32),
+            pltpu.SemaphoreType.DMA((CASES,)),
+        ],
         compiler_params=pltpu.CompilerParams(vmem_limit_bytes=12 << 20),
         name="final",
     )(
@@ -656,17 +642,18 @@
         jnp.asarray(force_table),
         jnp.asarray(weight_table),
         jnp.asarray(place_table),
+        state,
     )
 
 
 def per_device(displacement, load, home_slot, micro_state, state_slot, phases, phase_moduli):
     sent = run_pack(micro_state, state_slot, home_slot, displacement)
+    me = jnp.full((1, LANES), lax.axis_index(AXES), jnp.int32)
+    sent, me = lax.optimization_barrier((sent, me))
     received = exchange(sent.reshape(DEV, 1, WIDE)).reshape(DEV * CHUNKS, LANES)
-    answer, w, p, q, steps = run_solve(received, phases, phase_moduli, home_slot, load)
+    answer, state = run_solve(received, phases, phase_moduli, home_slot, load)
     returned = exchange(answer.reshape(DEV, 8, LANES)).reshape(DEV * 8, LANES)
-    new_state = run_update(w, p, q, steps)
-    me = jnp.full((1, LANES), lax.axis_index(AXES), jnp.int32)
-    displaced, residual, rel_norm = run_final(returned, me, displacement)
+    displaced, residual, rel_norm, new_state = run_final(returned, me, displacement, state)
     return (
         new_state.reshape(micro_state.shape),
         displaced,

time: 76.3 us -> 77.2 us (1.012)
  blocking collectives: 42.6 us -> 62.2 us
  Pallas kernels: 20.9 us -> 14.1 us
  starting transfers between devices: 6.32 us -> 0 us
  waiting for transfers between devices: 5.25 us -> 0 us
    all_to_all x1 -> x2, blocking collectives: 42.6 us -> 62.2 us  [exchange(): return lax.all_to_all(value, AXES, split_axis=0, concat_axis=0, tiled=True)]
    pallas_call x1 -> x0, Pallas kernels: 8.18 us -> none  [run_update(): pl.pallas_call(update_kernel, out_shape=jax.ShapeDtypeStruct((CASES, ROWS...]
    all_to_all x1 -> x0, starting transfers between devices: 6.32 us -> none  [exchange(): return lax.all_to_all(value, AXES, split_axis=0, concat_axis=0, tiled=True)]
    all_to_all x1 -> x0, waiting for transfers between devices: 5.25 us -> none  [exchange(): return lax.all_to_all(value, AXES, split_axis=0, concat_axis=0, tiled=True)]
    pallas_call x1, Pallas kernels: 1.79 us -> 2.88 us  [run_final(): pl.pallas_call(final_kernel, out_shape=(node_shape, node_shape, jax.Shape...]
  transfers between devices with their start and end apart: 1 -> 0, of which waited for: 1 -> 0; matrix products, arithmetic and copies ran while one was open for 0% -> 0% of each run, Pallas kernels for 11% -> 0%
where the time goes in v5:
time: 77.2 us; the launch traced here: 77.1 us
  blocking collectives  62.2 us (81%)
  Pallas kernels  14.1 us (18%)
    all_to_all x2, blocking collectives, exchange(): return lax.all_to_all(value, AXES, split_axis=0, concat_axis=0, tiled=True)  62.2 us
    pallas_call x1, Pallas kernels, run_solve(): pl.pallas_call(solve_kernel, out_shape=(jax.ShapeDtypeStruct((DEV * 8, LA...  8.23 us
    pallas_call x1, Pallas kernels, run_pack(): pl.pallas_call(pack_kernel, out_shape=jax.ShapeDtypeStruct((DEV * CHUNKS,...  2.94 us
    pallas_call x1, Pallas kernels, run_final(): pl.pallas_call(final_kernel, out_shape=(node_shape, node_shape, jax.Shape...  2.88 us

profile of v5, /device:TPU:1, one launch (start us, length us, event | category | flops | bytes accessed | tf_op | source)
XLA Modules:
  0.0 77.1 jit_solution(6417615807708970105)
XLA Ops:
  0.6 2.9 %pack.1 = f32[4608,128]{1,0:T(8,128)S(1)} custom-call(f32[4536,128]{1,0:T(8,128)} %bitcast.15, s32[1,128]{1,0:T(1,128)} %bitcast.16, s32[1,128]{1,0:T(1,128)} %bitcast.13, f32[3,1,2,8]{3,2,1,0:T(2,128)} %disp_ref.1), custom_call_target="tpu_custom_call" | custom-call | tf_op jit(solution)/shard_map/pack/pallas_call | solution.py:571
  3.6 0.0 copy-start.2
  3.6 0.0 copy-start.5
  3.6 0.0 copy-start.6
  3.6 0.0 copy-start.7
  3.6 42.6 %all_to_all.10 = f32[128,1,4608]{2,1,0:T(1,128)S(1)} all-to-all(f32[128,1,4608]{2,1,0:T(1,128)S(1)} %bitcast.10), channel_id=1, replica_groups=mesh['far'=16,'core'=2,'rve'=4] {'core','far','rve'}, dimensions={0} | all-to-all | bytes 4718592 | tf_op jit(solution)/shard_map/all_to_all | solution.py:567
  46.2 0.0 copy-start
  46.2 0.0 copy-start.1
  46.3 0.0 copy-start.3
  46.3 0.0 copy-start.4
  46.3 0.0 copy-done.2
  46.3 0.0 copy-done.5
  46.3 0.0 copy-done.6
  46.3 0.0 copy-done.7
  46.3 8.2 %solve.1 = (f32[1024,128]{1,0:T(8,128)S(1)}, f32[5192,128]{1,0:T(8,128)S(1)}) custom-call(f32[4608,128]{1,0:T(8,128)S(1)} %bitcast.9, s32[216,128]{1,0:T(8,128)S(1)} %copy-done.2, f32[2,3]{1,0:T(2,128)S(1)} %copy-done.7, s32[1,128]{1,0:T(1,128)S(1)} %bitcast.14, f32[3,1,2,8]{3,2,1,0:T(2,128)S(1)} %copy-done.5), custom_call_target="tpu_custom_call" | custom-call | tf_op jit(solution)/shard_map/solve/pallas_call | solution.py:596
  54.5 19.6 %all_to_all.11 = f32[128,8,128]{2,1,0:T(8,128)S(1)} all-to-all(f32[128,8,128]{2,1,0:T(8,128)S(1)} %bitcast.12), channel_id=1, replica_groups=mesh['far'=16,'core'=2,'rve'=4] {'core','far','rve'}, dimensions={0} | all-to-all | bytes 1048576 | tf_op jit(solution)/shard_map/all_to_all | solution.py:567
  74.2 0.0 copy-done
  74.2 0.0 copy-done.1
  74.2 0.0 copy-done.3
  74.2 0.0 copy-done.4
  74.2 2.9 %final.1 = (f32[3,1,2,8]{3,2,1,0:T(2,128)}, f32[3,1,2,8]{3,2,1,0:T(2,128)}, f32[1,1]{1,0:T(1,128)}, f32[7,648,128]{2,1,0:T(8,128)}) custom-call(f32[1024,128]{1,0:T(8,128)S(1)} %bitcast.11, s32[1,128]{1,0:T(1,128)S(1)} %broadcast_in_dim.3.me_ref, f32[3,1,2,8]{3,2,1,0:T(2,128)S(1)} %copy-done.4, f32[768,256]{1,0:T(8,128)S(1)} %copy-done, ...), custom_call_target="tpu_custom_call" | custom-call | tf_op jit(solution)/shard_map/final/pallas_call | solution.py:622
  (1 shorter events, 0.0 us)
Async XLA Ops:
  3.6 42.7 %copy-start.2 = (s32[216,128]{1,0:T(8,128)S(1)}, s32[216,128]{1,0:T(8,128)}, u32[]{:S(2)}) copy-start(s32[216,128]{1,0:T(8,128)} %phase_ref.1) | copy-start | bytes 331780
  3.6 42.7 %copy-start.5 = (f32[3,1,2,8]{3,2,1,0:T(2,128)S(1)}, f32[3,1,2,8]{3,2,1,0:T(2,128)}, u32[]{:S(2)}) copy-start(f32[3,1,2,8]{3,2,1,0:T(2,128)} %load_ref.1) | copy-start | bytes 580
  3.6 42.7 %copy-start.6 = (s32[128]{0:T(128)S(1)}, s32[128]{0:T(128)}, u32[]{:S(2)}) copy-start(s32[128]{0:T(128)} %param.12) | copy-start | bytes 1540
  3.6 42.7 %copy-start.7 = (f32[2,3]{1,0:T(2,128)S(1)}, f32[2,3]{1,0:T(2,128)}, u32[]{:S(2)}) copy-start(f32[2,3]{1,0:T(2,128)} %moduli_ref.1) | copy-start | bytes 76
  46.2 27.9 %copy-start = (f32[768,256]{1,0:T(8,128)S(1)}, f32[768,256]{1,0:T(8,128)}, u32[]{:S(2)}) copy-start(f32[768,256]{1,0:T(8,128)} %constant.24.clone.force_ref) | copy-start | bytes 2359300
  46.2 27.9 %copy-start.1 = (f32[4,128,128]{2,1,0:T(8,128)S(1)}, f32[4,128,128]{2,1,0:T(8,128)}, u32[]{:S(2)}) copy-start(f32[4,128,128]{2,1,0:T(8,128)} %constant.26.clone.place_ref) | copy-start | bytes 786436
  46.3 27.9 %copy-start.3 = (f32[144,128]{1,0:T(8,128)S(1)}, f32[144,128]{1,0:T(8,128)}, u32[]{:S(2)}) copy-start(f32[144,128]{1,0:T(8,128)} %constant.25.clone.weight_ref) | copy-start | bytes 221188
  46.3 27.9 %copy-start.4 = (f32[3,1,2,8]{3,2,1,0:T(2,128)S(1)}, f32[3,1,2,8]{3,2,1,0:T(2,128)}, u32[]{:S(2)}) copy-start(f32[3,1,2,8]{3,2,1,0:T(2,128)} %disp_ref.1) | copy-start | bytes 580

commit v6 on v4

--- a/solution.py
+++ b/solution.py
@@ -88,6 +88,13 @@
                     )
             place[az * 2 + (1 if row == 2 else 0), j, corner * 16 + row % 2 * 8 + col] = 1.0
     return force.reshape(6 * LANES, 2 * LANES), weights.reshape(18 * 8, LANES), place
+
+
+def split_table(table):
+    high = table.astype(jnp.bfloat16)
+    rest = table - high.astype(np.float32)
+    middle = rest.astype(jnp.bfloat16)
+    return high, middle, (rest - middle.astype(np.float32)).astype(jnp.bfloat16)
 
 
 def lane_iota(rows=1):
@@ -310,12 +317,11 @@
     )
     mu_ref[...] = mu
     mu2_ref[...] = mu + mu
-    w_ref[pl.ds(7, ROWS, stride=8), :] = jnp.zeros((ROWS, LANES), jnp.float32)
-    tail = None
     same = (sublane_iota(DEV) == lane_iota(DEV)).astype(jnp.float32).astype(jnp.bfloat16)
-    for k in range(CHUNKS):
+
+    def unpack(k):
         block = recv_ref[pl.ds(k, DEV, stride=CHUNKS), :]
-        turned = flip(same, block) if k % 3 == 1 else block.T
+        turned = flip(same, block) if k % 4 == 1 else block.T
         start, stop = k * LANES, min((k + 1) * LANES, CASES * ROWS)
         while start < stop:
             case = start // ROWS
@@ -324,9 +330,12 @@
                 start - k * LANES : end - k * LANES
             ]
             start = end
-        tail = turned
+        return turned
+
+    macro = macro_strain_rows(unpack(CHUNKS - 1))
+    for k in range(CHUNKS - 1):
+        unpack(k)
     saves[0].start()
-    macro = macro_strain_rows(tail)
     sub = sublane_iota()
     imposed = [
         jnp.where(sub == 0, macro[m], jnp.where(sub == m + 1, 1.0, 0.0)) for m in range(6)
@@ -502,13 +511,17 @@
         jnp.take_along_axis(recv_ref[pl.ds(m, DEV, stride=8), :].T, order, axis=1)
         for m in range(6)
     ]
-    forces = lax.dot_general(
-        jnp.concatenate(stress, axis=1),
-        force_ref[...],
-        (((1,), (0,)), ((), ())),
-        precision=HIGHEST,
-        preferred_element_type=jnp.float32,
-    )
+    parts = split_bf16(jnp.concatenate(stress, axis=1))
+    forces = None
+    for order_sum in (2, 1, 0):
+        for first in range(order_sum + 1):
+            product = lax.dot_general(
+                parts[first],
+                force_ref[order_sum - first],
+                (((1,), (0,)), ((), ())),
+                preferred_element_type=jnp.float32,
+            )
+            forces = product if forces is None else forces + product
     home = sublane_iota(DEV)
     upper = forces[:, LANES:]
     lifted = jnp.where(home < 64, pltpu.roll(upper, 68, 0), pltpu.roll(upper, 64, 0))
@@ -527,7 +540,7 @@
     left = jnp.where(me % 4 == 0, me + 3, me - 1)
     under = jnp.where(me >= 64, 64, jnp.where(me < 4, 0, -60))
     turned = special.T
-    diagonal = jnp.zeros((24, LANES), jnp.float32)
+    corners = []
     for k, source in enumerate((me, left, me - under, left - under)):
         picks = jnp.broadcast_to(row_of(order, source), (16, LANES))
         terms = jnp.take_along_axis(turned[64 + 16 * k : 80 + 16 * k], picks, axis=1)
@@ -538,12 +551,12 @@
                 at = (i * 6 + n) * 8
                 total = total + weight_ref[at : at + 8, :] * terms[t : t + 1]
             corner.append(total)
+        corners.append(jnp.concatenate(corner, axis=0))
+    pieces = split_bf16(jnp.concatenate(corners, axis=1))
+    diagonal = jnp.zeros((24, LANES), jnp.float32)
+    for piece in pieces:
         diagonal = diagonal + lax.dot_general(
-            jnp.concatenate(corner, axis=0),
-            place_ref[k],
-            (((1,), (0,)), ((), ())),
-            precision=HIGHEST,
-            preferred_element_type=jnp.float32,
+            piece, place_ref[...], (((1,), (0,)), ((), ())), preferred_element_type=jnp.float32
         )
     lane = lane_iota(8)
     same = lane // 16 == sublane_iota()
@@ -653,9 +666,9 @@
         returned,
         me,
         displacement,
-        jnp.asarray(force_table),
+        jnp.asarray(np.stack(split_table(force_table))),
         jnp.asarray(weight_table),
-        jnp.asarray(place_table),
+        jnp.asarray(place_table.reshape(4 * LANES, LANES), jnp.bfloat16),
     )
 
 

time: 76.3 us -> 75.9 us (level)
  no operation moved by 1% of the time
where the time goes in v6:
time: 75.9 us; the launch traced here: 75.5 us
  blocking collectives  42.6 us (56%)
  Pallas kernels  20.5 us (27%)
  starting transfers between devices  6.32 us (8%)
  waiting for transfers between devices  5.24 us (7%)
    all_to_all x1, blocking collectives, exchange(): return lax.all_to_all(value, AXES, split_axis=0, concat_axis=0, tiled=True)  42.6 us
    pallas_call x1, Pallas kernels, run_update(): pl.pallas_call(update_kernel, out_shape=jax.ShapeDtypeStruct((CASES, ROWS...  8.2 us
    pallas_call x1, Pallas kernels, run_solve(): pl.pallas_call(solve_kernel, out_shape=(jax.ShapeDtypeStruct((DEV * 8, LA...  7.7 us
    all_to_all x1, starting transfers between devices, exchange(): return lax.all_to_all(value, AXES, split_axis=0, concat_axis=0, tiled=True)  6.32 us
    all_to_all x1, waiting for transfers between devices, exchange(): return lax.all_to_all(value, AXES, split_axis=0, concat_axis=0, tiled=True)  5.24 us
    pallas_call x1, Pallas kernels, run_pack(): pl.pallas_call(pack_kernel, out_shape=jax.ShapeDtypeStruct((DEV * CHUNKS,...  2.94 us
    pallas_call x1, Pallas kernels, run_final(): pl.pallas_call(final_kernel, out_shape=(node_shape, node_shape, jax.Shape...  1.69 us
  transfers between devices with their start and end apart: 1, of which 1 were waited for; matrix products, arithmetic and copies ran while one was open for 0% of the time, Pallas kernels for 11%

profile of v6, /device:TPU:1, one launch (start us, length us, event | category | flops | bytes accessed | tf_op | source)
XLA Modules:
  0.0 75.5 jit_solution(3765010640061284444)
XLA Ops:
  0.6 2.9 %pack.1 = f32[4608,128]{1,0:T(8,128)S(1)} custom-call(f32[4536,128]{1,0:T(8,128)} %bitcast.15, s32[1,128]{1,0:T(1,128)} %bitcast.16, s32[1,128]{1,0:T(1,128)} %bitcast.12, f32[3,1,2,8]{3,2,1,0:T(2,128)} %disp_ref.1), custom_call_target="tpu_custom_call" | custom-call | tf_op jit(solution)/shard_map/pack/pallas_call | solution.py:585
  3.6 0.0 copy-start.2
  3.6 0.0 copy-start.5
  3.6 0.0 copy-start.6
  3.6 0.0 copy-start.7
  3.6 42.6 %all_to_all.10 = f32[128,1,4608]{2,1,0:T(1,128)S(1)} all-to-all(f32[128,1,4608]{2,1,0:T(1,128)S(1)} %bitcast.10), channel_id=1, replica_groups=mesh['far'=16,'core'=2,'rve'=4] {'core','far','rve'}, dimensions={0} | all-to-all | bytes 4718592 | tf_op jit(solution)/shard_map/all_to_all | solution.py:581
  46.2 0.0 copy-done.2
  46.2 0.0 copy-done.5
  46.2 0.0 copy-done.6
  46.2 0.0 copy-done.7
  46.2 7.7 %solve.1 = (f32[1024,128]{1,0:T(8,128)}, f32[5184,128]{1,0:T(8,128)}, f32[5184,128]{1,0:T(8,128)}, f32[5184,128]{1,0:T(8,128)}, f32[16,128]{1,0:T(8,128)S(1)}) custom-call(f32[4608,128]{1,0:T(8,128)S(1)} %bitcast.9, s32[216,128]{1,0:T(8,128)S(1)} %copy-done.2, f32[2,3]{1,0:T(2,128)S(1)} %copy-done.7, s32[1,128]{1,0:T(1,128)S(1)} %bitcast.13, ...), custom_call_target="tpu_custom_call" | custom-call | tf_op jit(solution)/shard_map/solve/pallas_call | solution.py:611
  54.0 6.3 %all-to-all-start.1 = ((f32[128,8,128]{2,1,0:T(8,128)}), f32[128,8,128]{2,1,0:T(8,128)S(1)}, u32[]{:S(2)}, u32[]{:S(2)}) async-start(f32[128,8,128]{2,1,0:T(8,128)} %bitcast.6), calls=%async_computation.1 | async-start | bytes 1048576 | tf_op jit(solution)/shard_map/all_to_all | solution.py:581
  60.3 0.0 copy-start
  60.3 0.0 copy-start.1
  60.3 0.0 copy-start.3
  60.3 0.0 copy-start.4
  60.3 8.2 %update.1 = f32[7,648,128]{2,1,0:T(8,128)} custom-call(f32[5184,128]{1,0:T(8,128)} %get-tuple-element.12.w_ref, f32[5184,128]{1,0:T(8,128)} %get-tuple-element.13.p_ref, f32[5184,128]{1,0:T(8,128)} %get-tuple-element.14.q_ref, f32[16,128]{1,0:T(8,128)S(1)} %get-tuple-element.15.step_ref), custom_call_target="tpu_custom_call" | custom-call | flops 20000000 | bytes 10000000 | tf_op jit(solution)/shard_map/update/pallas_call | solution.py:639
  68.5 5.2 %all-to-all-done.1 = f32[128,8,128]{2,1,0:T(8,128)S(1)} async-done(((f32[128,8,128]{2,1,0:T(8,128)}), f32[128,8,128]{2,1,0:T(8,128)S(1)}, u32[]{:S(2)}, u32[]{:S(2)}) %all-to-all-start.1) | async-done | bytes 524320 | tf_op jit(solution)/shard_map/all_to_all | solution.py:581
  73.8 0.0 copy-done
  73.8 0.0 copy-done.1
  73.8 0.0 copy-done.3
  73.8 0.0 copy-done.4
  73.8 1.7 %final.1 = (f32[3,1,2,8]{3,2,1,0:T(2,128)}, f32[3,1,2,8]{3,2,1,0:T(2,128)}, f32[1,1]{1,0:T(1,128)}) custom-call(f32[1024,128]{1,0:T(8,128)S(1)} %bitcast.11, s32[1,128]{1,0:T(1,128)S(1)} %broadcast_in_dim.3.me_ref, f32[3,1,2,8]{3,2,1,0:T(2,128)S(1)} %copy-done.4, bf16[3,768,256]{2,1,0:T(8,128)(2,1)S(1)} %copy-done, f32[144,128]{1,0:T(8,128)S(1)} %copy-done.3, ...), custom_call_target="tpu_custom_call" | custom-call | tf_op jit(solution)/shard_map/final/pallas_call | solution.py:657
  (1 shorter events, 0.0 us)
Async XLA Ops:
  3.6 42.6 %copy-start.2 = (s32[216,128]{1,0:T(8,128)S(1)}, s32[216,128]{1,0:T(8,128)}, u32[]{:S(2)}) copy-start(s32[216,128]{1,0:T(8,128)} %phase_ref.1) | copy-start | bytes 331780
  3.6 42.6 %copy-start.5 = (f32[3,1,2,8]{3,2,1,0:T(2,128)S(1)}, f32[3,1,2,8]{3,2,1,0:T(2,128)}, u32[]{:S(2)}) copy-start(f32[3,1,2,8]{3,2,1,0:T(2,128)} %load_ref.1) | copy-start | bytes 580
  3.6 42.6 %copy-start.6 = (s32[128]{0:T(128)S(1)}, s32[128]{0:T(128)}, u32[]{:S(2)}) copy-start(s32[128]{0:T(128)} %param.12) | copy-start | bytes 1540
  3.6 42.6 %copy-start.7 = (f32[2,3]{1,0:T(2,128)S(1)}, f32[2,3]{1,0:T(2,128)}, u32[]{:S(2)}) copy-start(f32[2,3]{1,0:T(2,128)} %moduli_ref.1) | copy-start | bytes 76
  54.0 19.8 %all-to-all-start.1 = ((f32[128,8,128]{2,1,0:T(8,128)}), f32[128,8,128]{2,1,0:T(8,128)S(1)}, u32[]{:S(2)}, u32[]{:S(2)}) async-start(f32[128,8,128]{2,1,0:T(8,128)} %bitcast.6), calls=%async_computation.1 | async-start | bytes 1048576 | tf_op jit(solution)/shard_map/all_to_all | solution.py:581
  60.3 13.5 %copy-start = (bf16[3,768,256]{2,1,0:T(8,128)(2,1)S(1)}, bf16[3,768,256]{2,1,0:T(8,128)(2,1)}, u32[]{:S(2)}) copy-start(bf16[3,768,256]{2,1,0:T(8,128)(2,1)} %constant.24.clone.force_ref) | copy-start | bytes 3538948
  60.3 13.5 %copy-start.1 = (bf16[512,128]{1,0:T(8,128)(2,1)S(1)}, bf16[512,128]{1,0:T(8,128)(2,1)}, u32[]{:S(2)}) copy-start(bf16[512,128]{1,0:T(8,128)(2,1)} %constant.26.clone.place_ref) | copy-start | bytes 393220
  60.3 13.5 %copy-start.3 = (f32[144,128]{1,0:T(8,128)S(1)}, f32[144,128]{1,0:T(8,128)}, u32[]{:S(2)}) copy-start(f32[144,128]{1,0:T(8,128)} %constant.25.clone.weight_ref) | copy-start | bytes 221188
  60.3 13.5 %copy-start.4 = (f32[3,1,2,8]{3,2,1,0:T(2,128)S(1)}, f32[3,1,2,8]{3,2,1,0:T(2,128)}, u32[]{:S(2)}) copy-start(f32[3,1,2,8]{3,2,1,0:T(2,128)} %disp_ref.1) | copy-start | bytes 580

commit v7 on v6

--- a/solution.py
+++ b/solution.py
@@ -33,9 +33,9 @@
 VMEM = pl.BlockSpec(memory_space=pltpu.VMEM)
 SMEM = pl.BlockSpec(memory_space=pltpu.SMEM)
 HBM = pl.BlockSpec(memory_space=pltpu.HBM)
-CUTS = (0, 6, 36)
+CUTS = (0, 4, 36)
 PARTS = len(CUTS) - 1
-STEP = 6
+STEP = 4
 UPDATE = 72
 
 
@@ -676,7 +676,7 @@
     sent = run_pack(micro_state, state_slot, home_slot, displacement)
     received = exchange(sent.reshape(DEV, 1, WIDE)).reshape(DEV * CHUNKS, LANES)
     answer, w, p, q, steps = run_solve(received, phases, phase_moduli, home_slot, load)
-    returned = exchange(answer.reshape(DEV, 8, LANES)).reshape(DEV * 8, LANES)
+    returned = exchange(answer.reshape(DEV, 1, 8 * LANES)).reshape(DEV * 8, LANES)
     new_state = run_update(w, p, q, steps)
     me = jnp.full((1, LANES), lax.axis_index(AXES), jnp.int32)
     displaced, residual, rel_norm = run_final(returned, me, displacement)

time: 75.9 us -> 75.8 us (level)
  no operation moved by 1% of the time
where the time goes in v7:
time: 75.8 us; the launch traced here: 75.4 us
  blocking collectives  42.6 us (56%)
  Pallas kernels  20.5 us (27%)
  starting transfers between devices  6.32 us (8%)
  waiting for transfers between devices  5.24 us (7%)
    all_to_all x1, blocking collectives, exchange(): return lax.all_to_all(value, AXES, split_axis=0, concat_axis=0, tiled=True)  42.6 us
    pallas_call x1, Pallas kernels, run_update(): pl.pallas_call(update_kernel, out_shape=jax.ShapeDtypeStruct((CASES, ROWS...  8.2 us
    pallas_call x1, Pallas kernels, run_solve(): pl.pallas_call(solve_kernel, out_shape=(jax.ShapeDtypeStruct((DEV * 8, LA...  7.7 us
    all_to_all x1, starting transfers between devices, exchange(): return lax.all_to_all(value, AXES, split_axis=0, concat_axis=0, tiled=True)  6.32 us
    all_to_all x1, waiting for transfers between devices, exchange(): return lax.all_to_all(value, AXES, split_axis=0, concat_axis=0, tiled=True)  5.24 us
    pallas_call x1, Pallas kernels, run_pack(): pl.pallas_call(pack_kernel, out_shape=jax.ShapeDtypeStruct((DEV * CHUNKS,...  2.89 us
    pallas_call x1, Pallas kernels, run_final(): pl.pallas_call(final_kernel, out_shape=(node_shape, node_shape, jax.Shape...  1.69 us
  transfers between devices with their start and end apart: 1, of which 1 were waited for; matrix products, arithmetic and copies ran while one was open for 0% of the time, Pallas kernels for 11%

profile of v7, /device:TPU:1, one launch (start us, length us, event | category | flops | bytes accessed | tf_op | source)
XLA Modules:
  0.0 75.4 jit_solution(4124352276517672824)
XLA Ops:
  0.6 2.9 %pack.1 = f32[4608,128]{1,0:T(8,128)S(1)} custom-call(f32[4536,128]{1,0:T(8,128)} %bitcast.15, s32[1,128]{1,0:T(1,128)} %bitcast.16, s32[1,128]{1,0:T(1,128)} %bitcast.12, f32[3,1,2,8]{3,2,1,0:T(2,128)} %disp_ref.1), custom_call_target="tpu_custom_call" | custom-call | tf_op jit(solution)/shard_map/pack/pallas_call | solution.py:585
  3.5 0.0 copy-start.2
  3.5 0.0 copy-start.5
  3.6 0.0 copy-start.6
  3.6 0.0 copy-start.7
  3.6 42.6 %all_to_all.10 = f32[128,1,4608]{2,1,0:T(1,128)S(1)} all-to-all(f32[128,1,4608]{2,1,0:T(1,128)S(1)} %bitcast.10), channel_id=1, replica_groups=mesh['far'=16,'core'=2,'rve'=4] {'core','far','rve'}, dimensions={0} | all-to-all | bytes 4718592 | tf_op jit(solution)/shard_map/all_to_all | solution.py:581
  46.2 0.0 copy-done.2
  46.2 0.0 copy-done.5
  46.2 0.0 copy-done.6
  46.2 0.0 copy-done.7
  46.2 7.7 %solve.1 = (f32[1024,128]{1,0:T(8,128)}, f32[5184,128]{1,0:T(8,128)}, f32[5184,128]{1,0:T(8,128)}, f32[5184,128]{1,0:T(8,128)}, f32[16,128]{1,0:T(8,128)S(1)}) custom-call(f32[4608,128]{1,0:T(8,128)S(1)} %bitcast.9, s32[216,128]{1,0:T(8,128)S(1)} %copy-done.2, f32[2,3]{1,0:T(2,128)S(1)} %copy-done.7, s32[1,128]{1,0:T(1,128)S(1)} %bitcast.13, ...), custom_call_target="tpu_custom_call" | custom-call | tf_op jit(solution)/shard_map/solve/pallas_call | solution.py:611
  53.9 6.3 %all-to-all-start.1 = ((f32[128,1,1024]{2,1,0:T(1,128)}), f32[128,1,1024]{2,1,0:T(1,128)S(1)}, u32[]{:S(2)}, u32[]{:S(2)}) async-start(f32[128,1,1024]{2,1,0:T(1,128)} %bitcast.6), calls=%async_computation.1 | async-start | bytes 1048576 | tf_op jit(solution)/shard_map/all_to_all | solution.py:581
  60.2 0.0 copy-start
  60.3 0.0 copy-start.1
  60.3 0.0 copy-start.3
  60.3 0.0 copy-start.4
  60.3 8.2 %update.1 = f32[7,648,128]{2,1,0:T(8,128)} custom-call(f32[5184,128]{1,0:T(8,128)} %get-tuple-element.12.w_ref, f32[5184,128]{1,0:T(8,128)} %get-tuple-element.13.p_ref, f32[5184,128]{1,0:T(8,128)} %get-tuple-element.14.q_ref, f32[16,128]{1,0:T(8,128)S(1)} %get-tuple-element.15.step_ref), custom_call_target="tpu_custom_call" | custom-call | flops 20000000 | bytes 10000000 | tf_op jit(solution)/shard_map/update/pallas_call | solution.py:639
  68.5 5.2 %all-to-all-done.1 = f32[128,1,1024]{2,1,0:T(1,128)S(1)} async-done(((f32[128,1,1024]{2,1,0:T(1,128)}), f32[128,1,1024]{2,1,0:T(1,128)S(1)}, u32[]{:S(2)}, u32[]{:S(2)}) %all-to-all-start.1) | async-done | bytes 524320 | tf_op jit(solution)/shard_map/all_to_all | solution.py:581
  73.7 0.0 copy-done
  73.7 0.0 copy-done.1
  73.7 0.0 copy-done.3
  73.7 0.0 copy-done.4
  73.7 1.7 %final.1 = (f32[3,1,2,8]{3,2,1,0:T(2,128)}, f32[3,1,2,8]{3,2,1,0:T(2,128)}, f32[1,1]{1,0:T(1,128)}) custom-call(f32[1024,128]{1,0:T(8,128)S(1)} %bitcast.11, s32[1,128]{1,0:T(1,128)S(1)} %broadcast_in_dim.3.me_ref, f32[3,1,2,8]{3,2,1,0:T(2,128)S(1)} %copy-done.4, bf16[3,768,256]{2,1,0:T(8,128)(2,1)S(1)} %copy-done, f32[144,128]{1,0:T(8,128)S(1)} %copy-done.3, ...), custom_call_target="tpu_custom_call" | custom-call | tf_op jit(solution)/shard_map/final/pallas_call | solution.py:657
  (1 shorter events, 0.0 us)
Async XLA Ops:
  3.5 42.6 %copy-start.2 = (s32[216,128]{1,0:T(8,128)S(1)}, s32[216,128]{1,0:T(8,128)}, u32[]{:S(2)}) copy-start(s32[216,128]{1,0:T(8,128)} %phase_ref.1) | copy-start | bytes 331780
  3.5 42.6 %copy-start.5 = (f32[3,1,2,8]{3,2,1,0:T(2,128)S(1)}, f32[3,1,2,8]{3,2,1,0:T(2,128)}, u32[]{:S(2)}) copy-start(f32[3,1,2,8]{3,2,1,0:T(2,128)} %load_ref.1) | copy-start | bytes 580
  3.6 42.6 %copy-start.6 = (s32[128]{0:T(128)S(1)}, s32[128]{0:T(128)}, u32[]{:S(2)}) copy-start(s32[128]{0:T(128)} %param.12) | copy-start | bytes 1540
  3.6 42.6 %copy-start.7 = (f32[2,3]{1,0:T(2,128)S(1)}, f32[2,3]{1,0:T(2,128)}, u32[]{:S(2)}) copy-start(f32[2,3]{1,0:T(2,128)} %moduli_ref.1) | copy-start | bytes 76
  53.9 19.8 %all-to-all-start.1 = ((f32[128,1,1024]{2,1,0:T(1,128)}), f32[128,1,1024]{2,1,0:T(1,128)S(1)}, u32[]{:S(2)}, u32[]{:S(2)}) async-start(f32[128,1,1024]{2,1,0:T(1,128)} %bitcast.6), calls=%async_computation.1 | async-start | bytes 1048576 | tf_op jit(solution)/shard_map/all_to_all | solution.py:581
  60.2 13.5 %copy-start = (bf16[3,768,256]{2,1,0:T(8,128)(2,1)S(1)}, bf16[3,768,256]{2,1,0:T(8,128)(2,1)}, u32[]{:S(2)}) copy-start(bf16[3,768,256]{2,1,0:T(8,128)(2,1)} %constant.24.clone.force_ref) | copy-start | bytes 3538948
  60.3 13.5 %copy-start.1 = (bf16[512,128]{1,0:T(8,128)(2,1)S(1)}, bf16[512,128]{1,0:T(8,128)(2,1)}, u32[]{:S(2)}) copy-start(bf16[512,128]{1,0:T(8,128)(2,1)} %constant.26.clone.place_ref) | copy-start | bytes 393220
  60.3 13.5 %copy-start.3 = (f32[144,128]{1,0:T(8,128)S(1)}, f32[144,128]{1,0:T(8,128)}, u32[]{:S(2)}) copy-start(f32[144,128]{1,0:T(8,128)} %constant.25.clone.weight_ref) | copy-start | bytes 221188
  60.3 13.5 %copy-start.4 = (f32[3,1,2,8]{3,2,1,0:T(2,128)S(1)}, f32[3,1,2,8]{3,2,1,0:T(2,128)}, u32[]{:S(2)}) copy-start(f32[3,1,2,8]{3,2,1,0:T(2,128)} %disp_ref.1) | copy-start | bytes 580

commit v8 on v7

--- a/solution.py
+++ b/solution.py
@@ -393,7 +393,7 @@
                 line = below
             return tuple(sums), work
 
-        return lax.fori_loop(0, R, plane, ((zero,) * 6, zero), unroll=2)
+        return lax.fori_loop(0, R, plane, ((zero,) * 6, zero), unroll=3)
 
     def force_pass(src, finish, dst):
         def plane(a, carry):
@@ -418,7 +418,7 @@
                     last = [own[PAIRS[2][i]] for i in range(3)]
             return tuple(totals)
 
-        totals = lax.fori_loop(0, R, plane, (zero,) * 3, unroll=2)
+        totals = lax.fori_loop(0, R, plane, (zero,) * 3, unroll=3)
         return (totals[0] + totals[1]) + totals[2]
 
     mean0, _ = stress_pass(w_ref, imposed, True, False)
@@ -440,7 +440,7 @@
         save_plane(base)
         return carry
 
-    lax.fori_loop(0, R, direction, 0)
+    lax.fori_loop(0, R, direction, 0, unroll=3)
     length = square1 + ratio * square1
     mean2, work2 = stress_pass(q_ref, None, False, True)
     step1 = square1 / (work2 + STAB * length)

time: 75.8 us -> 75.7 us (level)
  no operation moved by 1% of the time
where the time goes in v8:
time: 75.7 us; the launch traced here: 75.4 us
  blocking collectives  42.6 us (56%)
  Pallas kernels  20.4 us (27%)
  starting transfers between devices  6.32 us (8%)
  waiting for transfers between devices  5.24 us (7%)
    all_to_all x1, blocking collectives, exchange(): return lax.all_to_all(value, AXES, split_axis=0, concat_axis=0, tiled=True)  42.6 us
    pallas_call x1, Pallas kernels, run_update(): pl.pallas_call(update_kernel, out_shape=jax.ShapeDtypeStruct((CASES, ROWS...  8.2 us
    pallas_call x1, Pallas kernels, run_solve(): pl.pallas_call(solve_kernel, out_shape=(jax.ShapeDtypeStruct((DEV * 8, LA...  7.62 us
    all_to_all x1, starting transfers between devices, exchange(): return lax.all_to_all(value, AXES, split_axis=0, concat_axis=0, tiled=True)  6.32 us
    all_to_all x1, waiting for transfers between devices, exchange(): return lax.all_to_all(value, AXES, split_axis=0, concat_axis=0, tiled=True)  5.24 us
    pallas_call x1, Pallas kernels, run_pack(): pl.pallas_call(pack_kernel, out_shape=jax.ShapeDtypeStruct((DEV * CHUNKS,...  2.89 us
    pallas_call x1, Pallas kernels, run_final(): pl.pallas_call(final_kernel, out_shape=(node_shape, node_shape, jax.Shape...  1.69 us
  transfers between devices with their start and end apart: 1, of which 1 were waited for; matrix products, arithmetic and copies ran while one was open for 0% of the time, Pallas kernels for 11%

profile of v8, /device:TPU:1, one launch (start us, length us, event | category | flops | bytes accessed | tf_op | source)
XLA Modules:
  0.0 75.4 jit_solution(12958525591434553601)
XLA Ops:
  0.6 2.9 %pack.1 = f32[4608,128]{1,0:T(8,128)S(1)} custom-call(f32[4536,128]{1,0:T(8,128)} %bitcast.15, s32[1,128]{1,0:T(1,128)} %bitcast.16, s32[1,128]{1,0:T(1,128)} %bitcast.12, f32[3,1,2,8]{3,2,1,0:T(2,128)} %disp_ref.1), custom_call_target="tpu_custom_call" | custom-call | tf_op jit(solution)/shard_map/pack/pallas_call | solution.py:585
  3.5 0.0 copy-start.2
  3.5 0.0 copy-start.5
  3.6 0.0 copy-start.6
  3.6 0.0 copy-start.7
  3.6 42.6 %all_to_all.10 = f32[128,1,4608]{2,1,0:T(1,128)S(1)} all-to-all(f32[128,1,4608]{2,1,0:T(1,128)S(1)} %bitcast.10), channel_id=1, replica_groups=mesh['far'=16,'core'=2,'rve'=4] {'core','far','rve'}, dimensions={0} | all-to-all | bytes 4718592 | tf_op jit(solution)/shard_map/all_to_all | solution.py:581
  46.2 0.0 copy-done.2
  46.2 0.0 copy-done.5
  46.2 0.0 copy-done.6
  46.2 0.0 copy-done.7
  46.2 7.6 %solve.1 = (f32[1024,128]{1,0:T(8,128)}, f32[5184,128]{1,0:T(8,128)}, f32[5184,128]{1,0:T(8,128)}, f32[5184,128]{1,0:T(8,128)}, f32[16,128]{1,0:T(8,128)S(1)}) custom-call(f32[4608,128]{1,0:T(8,128)S(1)} %bitcast.9, s32[216,128]{1,0:T(8,128)S(1)} %copy-done.2, f32[2,3]{1,0:T(2,128)S(1)} %copy-done.7, s32[1,128]{1,0:T(1,128)S(1)} %bitcast.13, ...), custom_call_target="tpu_custom_call" | custom-call | tf_op jit(solution)/shard_map/solve/pallas_call | solution.py:611
  53.8 6.3 %all-to-all-start.1 = ((f32[128,1,1024]{2,1,0:T(1,128)}), f32[128,1,1024]{2,1,0:T(1,128)S(1)}, u32[]{:S(2)}, u32[]{:S(2)}) async-start(f32[128,1,1024]{2,1,0:T(1,128)} %bitcast.6), calls=%async_computation.1 | async-start | bytes 1048576 | tf_op jit(solution)/shard_map/all_to_all | solution.py:581
  60.2 0.0 copy-start
  60.2 0.0 copy-start.1
  60.2 0.0 copy-start.3
  60.2 0.0 copy-start.4
  60.2 8.2 %update.1 = f32[7,648,128]{2,1,0:T(8,128)} custom-call(f32[5184,128]{1,0:T(8,128)} %get-tuple-element.12.w_ref, f32[5184,128]{1,0:T(8,128)} %get-tuple-element.13.p_ref, f32[5184,128]{1,0:T(8,128)} %get-tuple-element.14.q_ref, f32[16,128]{1,0:T(8,128)S(1)} %get-tuple-element.15.step_ref), custom_call_target="tpu_custom_call" | custom-call | flops 20000000 | bytes 10000000 | tf_op jit(solution)/shard_map/update/pallas_call | solution.py:639
  68.4 5.2 %all-to-all-done.1 = f32[128,1,1024]{2,1,0:T(1,128)S(1)} async-done(((f32[128,1,1024]{2,1,0:T(1,128)}), f32[128,1,1024]{2,1,0:T(1,128)S(1)}, u32[]{:S(2)}, u32[]{:S(2)}) %all-to-all-start.1) | async-done | bytes 524320 | tf_op jit(solution)/shard_map/all_to_all | solution.py:581
  73.6 0.0 copy-done
  73.7 0.0 copy-done.1
  73.7 0.0 copy-done.3
  73.7 0.0 copy-done.4
  73.7 1.7 %final.1 = (f32[3,1,2,8]{3,2,1,0:T(2,128)}, f32[3,1,2,8]{3,2,1,0:T(2,128)}, f32[1,1]{1,0:T(1,128)}) custom-call(f32[1024,128]{1,0:T(8,128)S(1)} %bitcast.11, s32[1,128]{1,0:T(1,128)S(1)} %broadcast_in_dim.3.me_ref, f32[3,1,2,8]{3,2,1,0:T(2,128)S(1)} %copy-done.4, bf16[3,768,256]{2,1,0:T(8,128)(2,1)S(1)} %copy-done, f32[144,128]{1,0:T(8,128)S(1)} %copy-done.3, ...), custom_call_target="tpu_custom_call" | custom-call | tf_op jit(solution)/shard_map/final/pallas_call | solution.py:657
  (1 shorter events, 0.0 us)
Async XLA Ops:
  3.5 42.6 %copy-start.2 = (s32[216,128]{1,0:T(8,128)S(1)}, s32[216,128]{1,0:T(8,128)}, u32[]{:S(2)}) copy-start(s32[216,128]{1,0:T(8,128)} %phase_ref.1) | copy-start | bytes 331780
  3.5 42.6 %copy-start.5 = (f32[3,1,2,8]{3,2,1,0:T(2,128)S(1)}, f32[3,1,2,8]{3,2,1,0:T(2,128)}, u32[]{:S(2)}) copy-start(f32[3,1,2,8]{3,2,1,0:T(2,128)} %load_ref.1) | copy-start | bytes 580
  3.6 42.6 %copy-start.6 = (s32[128]{0:T(128)S(1)}, s32[128]{0:T(128)}, u32[]{:S(2)}) copy-start(s32[128]{0:T(128)} %param.12) | copy-start | bytes 1540
  3.6 42.6 %copy-start.7 = (f32[2,3]{1,0:T(2,128)S(1)}, f32[2,3]{1,0:T(2,128)}, u32[]{:S(2)}) copy-start(f32[2,3]{1,0:T(2,128)} %moduli_ref.1) | copy-start | bytes 76
  53.8 19.8 %all-to-all-start.1 = ((f32[128,1,1024]{2,1,0:T(1,128)}), f32[128,1,1024]{2,1,0:T(1,128)S(1)}, u32[]{:S(2)}, u32[]{:S(2)}) async-start(f32[128,1,1024]{2,1,0:T(1,128)} %bitcast.6), calls=%async_computation.1 | async-start | bytes 1048576 | tf_op jit(solution)/shard_map/all_to_all | solution.py:581
  60.2 13.5 %copy-start = (bf16[3,768,256]{2,1,0:T(8,128)(2,1)S(1)}, bf16[3,768,256]{2,1,0:T(8,128)(2,1)}, u32[]{:S(2)}) copy-start(bf16[3,768,256]{2,1,0:T(8,128)(2,1)} %constant.24.clone.force_ref) | copy-start | bytes 3538948
  60.2 13.5 %copy-start.1 = (bf16[512,128]{1,0:T(8,128)(2,1)S(1)}, bf16[512,128]{1,0:T(8,128)(2,1)}, u32[]{:S(2)}) copy-start(bf16[512,128]{1,0:T(8,128)(2,1)} %constant.26.clone.place_ref) | copy-start | bytes 393220
  60.2 13.5 %copy-start.3 = (f32[144,128]{1,0:T(8,128)S(1)}, f32[144,128]{1,0:T(8,128)}, u32[]{:S(2)}) copy-start(f32[144,128]{1,0:T(8,128)} %constant.25.clone.weight_ref) | copy-start | bytes 221188
  60.2 13.5 %copy-start.4 = (f32[3,1,2,8]{3,2,1,0:T(2,128)S(1)}, f32[3,1,2,8]{3,2,1,0:T(2,128)}, u32[]{:S(2)}) copy-start(f32[3,1,2,8]{3,2,1,0:T(2,128)} %disp_ref.1) | copy-start | bytes 580
